TPU v7x, 32 devices: a whole 2x2x4 slice. The times are simulated.
32 devices in a mesh: grp: 2 (over x), tm: 16 (over z, y, core).
Axes of the slice: x: 2, y: 2, z: 4, core: 2. Of those that a mesh axis runs over, the one named last changes fastest.
Arguments:
- visibilities: float32 [2048, 2, 16, 1024], P('tm', None, 'grp'), parts along dimension 2, may hold values from -6 to 6
- redundancy: int32 [2048], P('grp'), parts along dimension 0, may hold values from 0 to 511, as said below
- mode_counts: int32 [2048], P('tm'), may hold values from 4 to 16
- filters: bfloat16 [2048, 2, 16, 16, 512], P('tm', None, None, 'grp'), parts along dimension 3, may hold values from -0.0625 to 0.0625
Outputs:
- mmodes: float32 [2048, 2, 16, 512], P('tm', None, 'grp'), parts along dimension 2
- modes: float32 [2048, 2, 32], P('tm', None, 'grp'), parts along dimension 2
There are 2 independent parts, one for each index of `grp`. A program takes and returns all parts, laid end to end along the dimension named above; an argument that names none is the same for every part. Nothing has to cross between parts.
Inputs may be any that keep to these rules, and one draw needn't show every extreme that they name: `redundancy`: each of the 512 unique baselines is named by at least one raw baseline.
All inputs are finite; a program needn't handle non-finite values.
Results may differ from a plain program's by a relative error of at most 0.0029.
Values sent between devices are 32-bit elements; how exact they have to be, the bound alone decides.
A program may use at most 128 MiB of HBM per device.

v0:
```python
import functools

import numpy as np
import jax
import jax.numpy as jnp
from jax import lax
from jax.experimental import pallas as pl
from jax.experimental.pallas import tpu as pltpu
from jax.sharding import PartitionSpec as P

MESH = pl.DeviceIdType.MESH
LANES = 128
BLOCKS = 4
NT = (((1,), (1,)), ((), ()))


def split_bf16(x):
    high = x.astype(jnp.bfloat16)
    return high, (x - high.astype(jnp.float32)).astype(jnp.bfloat16)


def cmul_const(z, c):
    re, im = z
    if c == 1:
        return z
    if c == -1j:
        return im, -re
    cr, ci = float(c.real), float(c.imag)
    if abs(abs(cr) - abs(ci)) < 1e-12:
        return (re - im) * cr if ci * cr > 0 else (re + im) * cr, (re + im) * cr if ci * cr > 0 else (im - re) * cr
    return re * cr - im * ci, re * ci + im * cr


def small_fft(zs):
    n = len(zs)
    if n == 1:
        return zs
    half = n // 2
    tops = [(a[0] + b[0], a[1] + b[1]) for a, b in zip(zs[:half], zs[half:])]
    lows = [(a[0] - b[0], a[1] - b[1]) for a, b in zip(zs[:half], zs[half:])]
    turned = []
    for i, z in enumerate(lows):
        if i == 0:
            c = 1
        elif 4 * i == n:
            c = -1j
        else:
            c = np.exp(-2j * np.pi * i / n)
        turned.append(cmul_const(z, c))
    even, odd = small_fft(tops), small_fft(turned)
    out = [None] * n
    out[0::2], out[1::2] = even, odd
    return out


def rounded(x):
    return x.astype(jnp.bfloat16).astype(jnp.float32)[None]


def late_tiles(n, chans, uniq):
    halves = uniq // (n // chans) // LANES
    return [t for t in range(uniq // LANES) if t % halves]


def tables(groups, local):
    length = groups * local
    s = np.arange(local, dtype=np.int64)
    base = 2 * np.pi * (np.outer(s, s) % local) / local
    turn = 2 * np.pi * np.outer(np.arange(groups, dtype=np.int64), s) / length
    scale = length ** -0.5
    f32 = lambda a: jnp.asarray(a.astype(np.float32))
    return (
        f32(np.cos(base) * scale),
        f32(np.sin(base) * scale),
        f32(np.cos(turn).reshape(groups, 1, local)),
        f32(np.sin(turn).reshape(groups, 1, local)),
    )


def exchange_kernel(
    n, local, chans, uniq, kept,
    vis_ref, filt_ref, red_ref, cb_ref, sb_ref, tc_ref, ts_ref, out_ref, part_ref,
    vis_buf, wt, avg, send1, recv1, spec, mh, ml, send2, filt, got, lay, part,
    load_sem, s1_sem, r1_sem, s2_sem, r2_sem, own1_sem, own2_sem, filt_sem, got_sem, part_sem,
):
    me = lax.axis_index("tm")
    halves = uniq // (n // chans) // LANES
    per_chan = n // chans
    tb = local // BLOCKS
    rows = tb * 2 * chans
    keep = local // n

    def load(i):
        return pltpu.make_async_copy(
            vis_ref.at[pl.ds(i * rows, rows), :], vis_buf.at[i], load_sem.at[i]
        )

    for i in range(BLOCKS):
        load(i).start()

    barrier = pltpu.get_barrier_semaphore()

    def greet(o, carry):
        pl.semaphore_signal(
            barrier, inc=1, device_id={"tm": lax.rem(me + o, n)}, device_id_type=MESH
        )
        return carry

    lax.fori_loop(1, n, greet, 0)

    wt[...] = (
        lax.broadcasted_iota(jnp.int32, wt.shape, 0) == red_ref[...]
    ).astype(jnp.float32).astype(jnp.bfloat16)
    ones = jnp.ones((8, wt.shape[1]), jnp.bfloat16)
    counts = lax.dot_general(ones, wt[...], NT, preferred_element_type=jnp.float32)
    inverse = 1.0 / counts[0:1]

    def slot(dest, h):
        return lax.rem(dest, per_chan) * halves + h, lax.div(dest, per_chan)

    def first(o, h, i):
        dest = lax.rem(me + o, n)
        lane_tile, chan = slot(dest, h)
        if h == 0:
            span = pl.ds(i * tb, tb)
            q = i
        else:
            span = pl.ds(0, local)
            q = BLOCKS + h - 1
        return pltpu.make_async_remote_copy(
            src_ref=send1.at[lane_tile, chan, :, span, :],
            dst_ref=recv1.at[h, me, :, span, :],
            send_sem=s1_sem.at[o, q],
            recv_sem=r1_sem.at[o, q],
            device_id={"tm": dest},
            device_id_type=MESH,
        )

    def own_first(h):
        lane_tile, chan = slot(me, h)
        return pltpu.make_async_copy(
            send1.at[lane_tile, chan], recv1.at[h, me], own1_sem.at[h]
        )

    def each(f):
        def body(o, carry):
            f(o)
            return carry
        lax.fori_loop(1, n, body, 0)

    for i in range(BLOCKS):
        load(i).wait()
        high, low = split_bf16(vis_buf[i])
        summed = lax.dot_general(high, wt[...], NT, preferred_element_type=jnp.float32)
        summed += lax.dot_general(low, wt[...], NT, preferred_element_type=jnp.float32)
        mean = summed * inverse
        for lt in range(uniq // LANES):
            avg[lt] = mean[:, lt * LANES:(lt + 1) * LANES]
        for lt in range(uniq // LANES):
            for f in range(chans):
                for p in range(2):
                    send1[lt, f, p, i * tb:(i + 1) * tb, :] = avg[
                        lt, pl.ds(p * chans + f, tb, stride=2 * chans), :
                    ]
        if i == 0:
            pl.semaphore_wait(barrier, n - 1)
        each(lambda o: first(o, 0, i).start())
    for h in range(1, halves):
        each(lambda o: first(o, h, 0).start())
    for h in range(halves):
        own_first(h).start()

    def fetch(k, c):
        return pltpu.make_async_copy(
            filt_ref.at[pl.ds(k * n, n), :, :, :, pl.ds(c * halves * LANES, LANES)],
            filt.at[k, c],
            filt_sem.at[k, c],
        )

    for k in range(keep):
        for c in range(per_chan):
            fetch(k, c).start()

    def make_matrix(e, carry):
        cosine = cb_ref[...] * tc_ref[e] - sb_ref[...] * ts_ref[e]
        sine = sb_ref[...] * tc_ref[e] + cb_ref[...] * ts_ref[e]
        ch, cl = split_bf16(cosine)
        sh, sl = split_bf16(sine)
        for target, c, s in ((mh, ch, sh), (ml, cl, sl)):
            target[e, 0:local, 0:local] = c
            target[e, 0:local, local:] = s
            target[e, local:, 0:local] = -s
            target[e, local:, local:] = c
        return carry

    lax.fori_loop(0, n, make_matrix, 0)

    def second(o, h):
        dest = lax.rem(me + o, n)
        return pltpu.make_async_remote_copy(
            src_ref=send2.at[h, dest],
            dst_ref=out_ref.at[h, me],
            send_sem=s2_sem.at[o, h],
            recv_sem=r2_sem.at[o, h],
            device_id={"tm": dest},
            device_id_type=MESH,
        )

    def own_second(h):
        return pltpu.make_async_copy(send2.at[h, me], out_ref.at[h, me], own2_sem.at[h])

    for h in range(halves):
        own_first(h).wait()
        if h == 0:
            for i in range(BLOCKS):
                each(lambda o: first(o, 0, i).wait_recv())
        else:
            each(lambda o: first(o, h, 0).wait_recv())

        def across(g, carry):
            at = pl.ds(pl.multiple_of(g * 8, 8), 8)
            zs = [(recv1[h, d, 0, at, :], recv1[h, d, 1, at, :]) for d in range(n)]
            for e, (re, im) in enumerate(small_fft(zs)):
                spec[e, 0, at, :] = re
                spec[e, 1, at, :] = im
            return carry

        lax.fori_loop(0, local // 8, across, 0)

        def within(e, carry):
            high, low = split_bf16(spec[e].reshape(2 * local, LANES))
            dot = functools.partial(jnp.dot, preferred_element_type=jnp.float32)
            value = dot(mh[e], high) + (dot(mh[e], low) + dot(ml[e], high))
            value = value.reshape(2, n, keep, LANES)
            for p in range(2):
                send2[h, :, e, p] = value[p]
            return carry

        lax.fori_loop(0, n, within, 0)
        each(lambda o: second(o, h).start())
        own_second(h).start()

    own_second(0).wait()
    each(lambda o: second(o, 0).wait_recv())
    read = pltpu.make_async_copy(out_ref.at[0], got, got_sem)
    read.start()
    read.wait()
    width = n * 2 * chans

    def place(e, carry):
        for j in range(n):
            for p in range(2):
                start = (e * 2 + p) * chans + j // per_chan
                lay[j % per_chan, pl.ds(start, keep, stride=width), :] = got[j, e, p]
        return carry

    lax.fori_loop(0, n, place, 0)

    def early(k, carry):
        for c in range(per_chan):
            fetch(k, c).wait()

        def one(m, inner):
            at = pl.multiple_of(k * width + m * 2 * chans, 2 * chans)
            real = jnp.zeros((kept, chans, LANES), jnp.float32)
            imag = jnp.zeros((kept, chans, LANES), jnp.float32)
            for c in range(per_chan):
                x0 = rounded(lay[c, pl.ds(at, chans), :])
                x1 = rounded(lay[c, pl.ds(at + chans, chans), :])
                f0 = filt[k, c, m, 0].astype(jnp.float32)
                f1 = filt[k, c, m, 1].astype(jnp.float32)
                real += f0 * x0 - f1 * x1
                imag += f0 * x1 + f1 * x0
            part[k * n + m, 0] = jnp.sum(real, axis=1)
            part[k * n + m, 1] = jnp.sum(imag, axis=1)
            return inner

        lax.fori_loop(0, n, one, 0)
        return carry

    lax.fori_loop(0, keep, early, 0)
    save = pltpu.make_async_copy(part, part_ref, part_sem)
    save.start()

    for i in range(BLOCKS):
        each(lambda o: first(o, 0, i).wait_send())
    for h in range(1, halves):
        each(lambda o: first(o, h, 0).wait_send())
    each(lambda o: second(o, 0).wait_send())
    for h in range(1, halves):
        own_second(h).wait()
        each(lambda o: second(o, h).wait())
    save.wait()


def project_kernel(
    n, local, chans, uniq, kept, got_ref, early_ref, *refs
):
    late = late_tiles(n, chans, uniq)
    filt_refs = dict(zip(late, refs))
    mm_ref, modes_ref, lay, part = refs[len(late):]
    step = pl.program_id(0)
    per_chan = n // chans
    lane_tiles = uniq // LANES
    halves = lane_tiles // per_chan
    keep = local // n
    width = n * 2 * chans

    @pl.when(step == 0)
    def _():
        def place(e, carry):
            for h in range(halves):
                for j in range(n):
                    lt = (j % per_chan) * halves + h
                    for p in range(2):
                        start = (e * 2 + p) * chans + j // per_chan
                        lay[lt, pl.ds(start, keep, stride=width), :] = got_ref[h, j, e, p]
            return carry

        lax.fori_loop(0, n, place, 0)

    def one(m, carry):
        at = pl.multiple_of(step * width + m * 2 * chans, 2 * chans)
        real = jnp.zeros((kept, chans, LANES), jnp.float32)
        imag = jnp.zeros((kept, chans, LANES), jnp.float32)
        for lt in range(lane_tiles):
            cols = slice(lt * LANES, (lt + 1) * LANES)
            x0 = lay[lt, pl.ds(at, chans), :]
            x1 = lay[lt, pl.ds(at + chans, chans), :]
            mm_ref[m, 0, :, cols] = x0
            mm_ref[m, 1, :, cols] = x1
            if lt not in filt_refs:
                continue
            x0, x1 = rounded(x0), rounded(x1)
            f0 = filt_refs[lt][m, 0].astype(jnp.float32)
            f1 = filt_refs[lt][m, 1].astype(jnp.float32)
            real += f0 * x0 - f1 * x1
            imag += f0 * x1 + f1 * x0
        part[m, 0] = jnp.sum(real, axis=1) + early_ref[m, 0]
        part[m, 1] = jnp.sum(imag, axis=1) + early_ref[m, 1]
        return carry

    lax.fori_loop(0, n, one, 0)
    sums = part[...].reshape(n * 2 * kept, LANES)
    total = lax.dot_general(
        jnp.ones((8, LANES), jnp.float32), sums, NT,
        precision=lax.Precision.HIGHEST, preferred_element_type=jnp.float32,
    )
    modes_ref[0] = total[0:1]


def fits(n, local, chans, raw, uniq, kept):
    return (
        n % chans == 0
        and uniq % ((n // chans) * LANES) == 0
        and local % (8 * n) == 0
        and local % (8 * BLOCKS) == 0
        and local % LANES == 0
        and chans == 8
        and raw % LANES == 0
        and kept % 8 == 0
        and local == 8 * n
    )


def fused_device(visibilities, redundancy, mode_counts, filters):
    n = lax.axis_size("tm")
    local, _, chans, raw = visibilities.shape
    uniq, kept = filters.shape[4], filters.shape[2]
    halves = uniq // (n // chans) // LANES
    keep = local // n
    rows = local * 2 * chans
    vmem = pl.BlockSpec(memory_space=pltpu.VMEM)
    hbm = pl.BlockSpec(memory_space=pl.ANY)
    f32, bf16 = jnp.float32, jnp.bfloat16
    dma = pltpu.SemaphoreType.DMA
    per_chan = n // chans
    late = late_tiles(n, chans, uniq)
    got, early = pl.pallas_call(
        functools.partial(exchange_kernel, n, local, chans, uniq, kept),
        out_shape=(
            jax.ShapeDtypeStruct((halves, n, n, 2, keep, LANES), f32),
            jax.ShapeDtypeStruct((local, 2, kept, LANES), f32),
        ),
        in_specs=[hbm] * 2 + [vmem] * 5,
        out_specs=(hbm, hbm),
        scratch_shapes=[
            pltpu.VMEM((BLOCKS, rows // BLOCKS, raw), f32),
            pltpu.VMEM((uniq, raw), bf16),
            pltpu.VMEM((uniq // LANES, rows // BLOCKS, LANES), f32),
            pltpu.VMEM((uniq // LANES, chans, 2, local, LANES), f32),
            pltpu.VMEM((halves, n, 2, local, LANES), f32),
            pltpu.VMEM((n, 2, local, LANES), f32),
            pltpu.VMEM((n, 2 * local, 2 * local), bf16),
            pltpu.VMEM((n, 2 * local, 2 * local), bf16),
            pltpu.VMEM((halves, n, n, 2, keep, LANES), f32),
            pltpu.VMEM((keep, per_chan, n, 2, kept, chans, LANES), bf16),
            pltpu.VMEM((n, n, 2, keep, LANES), f32),
            pltpu.VMEM((per_chan, rows, LANES), f32),
            pltpu.VMEM((local, 2, kept, LANES), f32),
            dma((BLOCKS,)),
            dma((n, BLOCKS + halves - 1)),
            dma((n, BLOCKS + halves - 1)),
            dma((n, halves)),
            dma((n, halves)),
            dma((halves,)),
            dma((halves,)),
            dma((keep, per_chan)),
            dma,
            dma,
        ],
        compiler_params=pltpu.CompilerParams(
            collective_id=0, has_side_effects=True, vmem_limit_bytes=60 * 2**20
        ),
        name="exchange",
    )(visibilities.reshape(rows, raw), filters, redundancy.reshape(1, raw), *tables(n, local))
    width = n * 2 * chans
    mmodes, flat = pl.pallas_call(
        functools.partial(project_kernel, n, local, chans, uniq, kept),
        grid=(keep,),
        out_shape=(
            jax.ShapeDtypeStruct((local, 2, chans, uniq), f32),
            jax.ShapeDtypeStruct((keep, 1, n * 2 * kept), f32),
        ),
        in_specs=[
            pl.BlockSpec(got.shape, lambda k: (0,) * 6),
            pl.BlockSpec((n, 2, kept, LANES), lambda k: (k, 0, 0, 0)),
        ]
        + [
            pl.BlockSpec((n, 2, kept, chans, LANES), functools.partial(lambda t, k: (k, 0, 0, 0, t), t))
            for t in late
        ],
        out_specs=(
            pl.BlockSpec((n, 2, chans, uniq), lambda k: (k, 0, 0, 0)),
            pl.BlockSpec((1, 1, n * 2 * kept), lambda k: (k, 0, 0)),
        ),
        scratch_shapes=[
            pltpu.VMEM((uniq // LANES, keep * width, LANES), f32),
            pltpu.VMEM((n, 2, kept, LANES), f32),
        ],
        compiler_params=pltpu.CompilerParams(vmem_limit_bytes=56 * 2**20),
        name="project",
    )(got, early, *[filters] * len(late))
    coefs = flat.reshape(local, 2, kept)
    kept_mask = lax.broadcasted_iota(jnp.int32, (local, kept), 1) < mode_counts[:, None]
    return mmodes, jnp.where(kept_mask[:, None, :], coefs, 0.0)


def phase_table(numer, period):
    phases = 2.0 * jnp.pi / period * numer.astype(jnp.float32)
    return (jnp.cos(phases), jnp.sin(phases))


def apply_stacked(cosine, sine_table, stacked, width):
    cos_part = jnp.dot(
        cosine, stacked, precision=lax.Precision.HIGHEST, preferred_element_type=jnp.float32
    )
    sin_part = jnp.dot(
        sine_table, stacked, precision=lax.Precision.HIGHEST, preferred_element_type=jnp.float32
    )
    real_out = cos_part[:, :width] + sin_part[:, width:]
    imag_out = cos_part[:, width:] - sin_part[:, :width]
    return jnp.concatenate([real_out, imag_out], axis=1)


def factored_transform(stacked, width):
    length = stacked.shape[0]
    radix_size = 64
    inner_size = length // radix_size
    outer_row = lax.broadcasted_iota(jnp.int32, (radix_size, radix_size), 0)
    outer_col = lax.broadcasted_iota(jnp.int32, (radix_size, radix_size), 1)
    cosine, sine_table = phase_table(outer_row * outer_col % radix_size, radix_size)
    grouped = stacked.reshape(radix_size, inner_size, 2, width)
    grouped = jnp.transpose(grouped, (0, 2, 1, 3)).reshape(radix_size, 2 * inner_size * width)
    section = apply_stacked(cosine, sine_table, grouped, inner_size * width)
    section = section.reshape(radix_size, 2, inner_size, width)
    section_real = section[:, 0]
    section_imag = section[:, 1]
    twist_row = lax.broadcasted_iota(jnp.int32, (radix_size, inner_size, 1), 0)
    twist_col = lax.broadcasted_iota(jnp.int32, (radix_size, inner_size, 1), 1)
    twist_cos, twist_sin = phase_table(twist_row * twist_col, length)
    turned_real = section_real * twist_cos + section_imag * twist_sin
    turned_imag = section_imag * twist_cos - section_real * twist_sin
    turned = jnp.stack([turned_real, turned_imag], axis=0)
    turned = jnp.transpose(turned, (2, 0, 1, 3)).reshape(inner_size, 2 * radix_size * width)
    inner_row = lax.broadcasted_iota(jnp.int32, (inner_size, inner_size), 0)
    inner_col = lax.broadcasted_iota(jnp.int32, (inner_size, inner_size), 1)
    cosine2, sine_table2 = phase_table(inner_row * inner_col % inner_size, inner_size)
    final = apply_stacked(cosine2, sine_table2, turned, radix_size * width)
    final = final.reshape(inner_size, 2, radix_size, width)
    return jnp.transpose(final, (0, 2, 1, 3)).reshape(length, 2 * width)


def transform(columns):
    length, _, width = columns.shape
    stacked = columns.reshape(length, 2 * width)
    result = factored_transform(stacked, width)
    scale = 1.0 / jnp.sqrt(jnp.float32(length))
    return (result * scale).reshape(length, 2, width)


def on_device(visibilities, redundancy, mode_counts, filters):
    groups = lax.axis_size("tm")
    local_times, _, channels, raw_count = visibilities.shape
    uniques = filters.shape[4]
    kept = filters.shape[2]
    if fits(groups, local_times, channels, raw_count, uniques, kept):
        return fused_device(visibilities, redundancy, mode_counts, filters)
    unique_block = uniques // groups
    members = (
        redundancy[:, None] == lax.broadcasted_iota(jnp.int32, (raw_count, uniques), 1)
    ).astype(jnp.float32)
    weights = members / jnp.sum(members, axis=0, keepdims=True)
    flat_rows = visibilities.reshape(local_times, 2 * channels, raw_count)
    blocked_weights = weights.reshape(raw_count, groups, unique_block)
    packed = jnp.einsum(
        "tqr,rjc->tjqc",
        flat_rows,
        blocked_weights,
        precision=lax.Precision.HIGHEST,
        preferred_element_type=jnp.float32,
    )
    packed = packed.reshape(local_times, groups, 2 * channels * unique_block)
    arrived = lax.all_to_all(packed, "tm", split_axis=1, concat_axis=0, tiled=True)
    length = arrived.shape[0]
    spectra = transform(arrived.reshape(length, 2, channels * unique_block))
    spectra = spectra.reshape(length, 1, 2 * channels * unique_block)
    regrouped = lax.all_to_all(spectra, "tm", split_axis=0, concat_axis=1, tiled=True)
    regrouped = regrouped.reshape(local_times, groups, 2, channels, unique_block)
    mmodes = jnp.transpose(regrouped, (0, 2, 3, 1, 4)).reshape(local_times, 2, channels, uniques)
    local_modes = mmodes.shape[0]
    rounded = mmodes.astype(jnp.bfloat16).reshape(local_modes, 2, channels * uniques)
    flat_filters = filters.reshape(local_modes, 2, kept, channels * uniques)
    products = jnp.einsum(
        "mpkc,mqc->mpqk", flat_filters, rounded, preferred_element_type=jnp.float32
    )
    real_out = products[:, 0, 0] - products[:, 1, 1]
    imag_out = products[:, 0, 1] + products[:, 1, 0]
    kept_mask = lax.broadcasted_iota(jnp.int32, (local_modes, kept), 1) < mode_counts[:, None]
    modes = jnp.where(kept_mask[:, None, :], jnp.stack([real_out, imag_out], axis=1), 0.0)
    return (mmodes, modes)


def solution(mesh):
    return jax.shard_map(
        on_device,
        mesh=mesh,
        in_specs=(P("tm", None, "grp", None), P("grp"), P("tm"), P("tm", None, None, "grp", None)),
        out_specs=(P("tm", None, "grp", None), P("tm", None, "grp")),
        check_vma=False,
    )
```

profile of v0, /device:TPU:13, one launch (start us, length us, event | category | flops | bytes accessed | tf_op | source)
XLA Modules:
  0.0 211.6 jit_solution(9821540934089472570)
XLA Ops:
  0.6 188.7 %exchange.1 = (f32[2,16,16,2,8,128]{5,4,3,2,1,0:T(8,128)}, f32[128,2,16,128]{3,2,1,0:T(8,128)}) custom-call(f32[2048,1024]{1,0:T(8,128)} %bitcast.2, bf16[128,2,16,8,512]{4,3,2,1,0:T(8,128)(2,1)} %refs_1_.1, s32[1,1024]{1,0:T(1,128)} %bitcast.3, f32[128,128]{1,0:T(8,128)} %constant.10.clone.cb_ref, f32[128,128]{1,0:T(8,128)} %constant.11.clone.sb_ref, ...), custom_call_target="tpu_custom_call" | custom-call | tf_op jit(solution)/shard_map/exchange/pallas_call | solution.py:379
  189.3 0.0 copy-start
  189.4 20.4 %project.1 = (f32[128,2,8,512]{3,2,1,0:T(8,128)}, f32[8,1,512]{2,1,0:T(1,128)}) custom-call(f32[2,16,16,2,8,128]{5,4,3,2,1,0:T(8,128)} %get-tuple-element.6.got_ref, f32[128,2,16,128]{3,2,1,0:T(8,128)} %get-tuple-element.7.early_ref, bf16[128,2,16,8,512]{4,3,2,1,0:T(8,128)(2,1)} %refs_1_.1, bf16[128,2,16,8,512]{4,3,2,1,0:T(8,128)(2,1)} %refs_1_.1), custom_call_target="tpu_custom_call" | custom-call | tf_op jit(solution)/shard_map/project/pallas_call | solution.py:418
  209.8 0.8 reduce
  210.5 0.2 reshape.30
  210.7 0.0 copy-done
  210.7 0.1 iota_compare_fusion
  210.8 0.1 broadcast_select_fusion
  210.9 0.7 copy.11
Async XLA Ops:
  189.3 21.4 %copy-start = (s32[128]{0:T(128)S(1)}, s32[128]{0:T(128)}, u32[]{:S(2)}) copy-start(s32[128]{0:T(128)} %param.10) | copy-start | bytes 1540
where the time goes:
time: 212 us
  Pallas kernels  209 us (99%)
    pallas_call x1, Pallas kernels, fused_device(): pl.pallas_call(functools.partial(exchange_kernel, n, local, chans, uniq,...  189 us
    pallas_call x1, Pallas kernels, fused_device(): pl.pallas_call(functools.partial(project_kernel, n, local, chans, uniq, k...  20.4 us

commit v1 on v0

v1 whole, which is shorter than its diff:
```python
import functools

import numpy as np
import jax
import jax.numpy as jnp
from jax import lax
from jax.experimental import pallas as pl
from jax.experimental.pallas import tpu as pltpu
from jax.sharding import PartitionSpec as P

MESH = pl.DeviceIdType.MESH
LANES = 128
BLOCKS = 4
RADIX = 4
NT = (((1,), (1,)), ((), ()))


def split_bf16(x):
    high = x.astype(jnp.bfloat16)
    return high, (x - high.astype(jnp.float32)).astype(jnp.bfloat16)


def rounded(x):
    return x.astype(jnp.bfloat16).astype(jnp.float32)[None]


def slab_factors(span, length):
    i = np.arange(span)
    side = np.sin(np.pi * (i[:-1] + 1) / length) * np.sin(np.pi * (span - 1 - i[:-1]) / length)
    middle = -np.cos(np.pi * (2 * i + 1 - span) / length) * np.cos(np.pi * span / length)
    _, basis = np.linalg.eigh(np.diag(middle) + np.diag(side, 1) + np.diag(side, -1))
    basis = basis[:, ::-1]
    mid = (span - 1) / 2
    at = i - mid
    basis = basis * np.where((1 + at / span) @ basis < 0, -1.0, 1.0)
    image = np.exp(-2j * np.pi / length * np.outer(at, at)) @ basis
    sizes = np.sqrt(np.sum(np.abs(image) ** 2, axis=0))
    rank = int(np.sum(sizes > sizes[0] * 2.0 ** -24))
    rank = -(-rank // 4) * 4
    dec = image[:, :rank] * np.exp(-2j * np.pi * mid / length * i)[:, None]
    enc = basis[:, :rank].T * np.exp(-2j * np.pi * mid / length * at)
    return dec, enc


def split_rows(rank):
    main = rank // 8 * 8
    return main, 2 * rank


def real_rows(re, im):
    main, _ = split_rows(re.shape[0])
    return np.concatenate([re[:main], im[:main], re[main:], im[main:]], axis=0)


def stacked_tables(slab, local):
    span = slab * local
    length = RADIX * span
    dec, enc = slab_factors(span, length)
    rank = enc.shape[0]
    rows = -(-2 * rank // 16) * 16
    deep = -(-2 * rank // LANES) * LANES
    per = local // RADIX
    bf16 = jnp.bfloat16

    def halves(a):
        high = a.astype(np.float32).astype(bf16)
        low = (a.astype(np.float32) - high.astype(np.float32)).astype(bf16)
        return np.concatenate([high, low], axis=0)

    enc_tables, dec_tables = [], []
    for r in range(RADIX):
        t = np.arange(span).reshape(slab, per, RADIX)[:, :, r]
        part = enc[:, t]
        cols = np.stack(
            [real_rows(part.real, part.imag), real_rows(-part.imag, part.real)], axis=2
        ).reshape(2 * rank, slab * 2 * per)
        enc_tables.append(halves(np.pad(cols, ((0, rows - 2 * rank), (0, 0)))))
        part = dec[t] * length ** -0.5
        part = np.moveaxis(part, -1, 0)
        cols = np.stack(
            [real_rows(part.real, -part.imag), real_rows(part.imag, part.real)], axis=2
        ).reshape(2 * rank, slab * 2 * per)
        dec_tables.append(halves(np.pad(cols, ((0, deep - 2 * rank), (0, 0))).T))
    return rank, jnp.asarray(np.stack(enc_tables)), jnp.asarray(np.stack(dec_tables))


def dft_radix(load, store, rank):
    main, total = split_rows(rank)

    def spread(g, turn):
        s02, d02 = g[0] + g[2], g[0] - g[2]
        s13, d13 = g[1] + g[3], turn(g[1] - g[3])
        return s02 + s13, d02 + d13, s02 - s13, d02 - d13

    def pair(q, carry):
        re = pl.ds(pl.multiple_of(q * 8, 8), 8)
        im = pl.ds(pl.multiple_of(main + q * 8, 8), 8)
        a = [load(k, re) for k in range(4)]
        b = [load(k, im) for k in range(4)]
        sa, da, sb, db = a[0] + a[2], a[0] - a[2], b[0] + b[2], b[0] - b[2]
        ta, ea, tb, eb = a[1] + a[3], a[1] - a[3], b[1] + b[3], b[1] - b[3]
        for k, (x, y) in enumerate(
            ((sa + ta, sb + tb), (da + eb, db - ea), (sa - ta, sb - tb), (da - eb, db + ea))
        ):
            store(k, re, x)
            store(k, im, y)
        return carry

    lax.fori_loop(0, main // 8, pair, 0, unroll=3)
    if total > 2 * main:
        at = pl.ds(2 * main, 8)
        sign = jnp.where(lax.broadcasted_iota(jnp.int32, (8, LANES), 0) < 4, 1.0, -1.0)
        out = spread([load(k, at) for k in range(4)], lambda v: pltpu.roll(v, 4, 0) * sign)
        for k in range(4):
            store(k, at, out[k])


def stacked_dot(table, x):
    high, low = split_bf16(x)
    out = jnp.dot(table, jnp.concatenate([high, low], axis=1), preferred_element_type=jnp.float32)
    out = out[:, :LANES] + out[:, LANES:]
    half = out.shape[0] // 2
    return out[:half] + out[half:]


def fused_kernel(
    n, local, chans, uniq, kept, rank,
    vis_ref, filt_ref, enc_hbm, dec_hbm, red_ref, mm_ref, modes_ref,
    vis_buf, wt, avg, send, recv_a, mix, send_b, recv_b, back, recv_c, lay, part, filt, enc, dec,
    load_sem, tab_sem, a0s, a0r, as_, ar, bs, br, cs, cr, filt_sem, out_sem,
):
    slab = n // RADIX
    me = lax.axis_index("tm")
    z, c = lax.div(me, slab), lax.rem(me, slab)
    tiles = uniq // LANES
    per_dev = chans // slab
    steps = tiles * per_dev
    tb = local // BLOCKS
    vb = tb // RADIX
    per = local // RADIX
    width = 2 * chans
    total = 2 * rank

    def load(i, r):
        return pltpu.make_async_copy(
            vis_ref.at[pl.ds(i * vb, vb), r], vis_buf.at[i, r], load_sem.at[i, r]
        )

    def fetch(j, slot):
        return pltpu.make_async_copy(
            filt_ref.at[:, :, :, :, pl.ds(pl.multiple_of(j * LANES, LANES), LANES)],
            filt.at[slot],
            filt_sem.at[slot],
        )

    table_copies = [
        pltpu.make_async_copy(enc_hbm, enc, tab_sem.at[0]),
        pltpu.make_async_copy(dec_hbm, dec, tab_sem.at[1]),
    ]
    for i in range(BLOCKS):
        for r in range(RADIX):
            load(i, r).start()
    for copy in table_copies:
        copy.start()

    def in_slab(o):
        return z * slab + lax.rem(c + o, slab)

    def across(o):
        return lax.rem(z + o, RADIX) * slab + c

    barrier = pltpu.get_barrier_semaphore()
    peers = [in_slab(o) for o in range(1, slab)] + [across(o) for o in range(1, RADIX)]
    for peer in peers:
        pl.semaphore_signal(barrier, inc=1, device_id={"tm": peer}, device_id_type=MESH)

    wt[...] = (
        lax.broadcasted_iota(jnp.int32, wt.shape, 0) == red_ref[...]
    ).astype(jnp.float32).astype(jnp.bfloat16)
    ones = jnp.ones((8, wt.shape[1]), jnp.bfloat16)
    counts = lax.dot_general(ones, wt[...], NT, preferred_element_type=jnp.float32)
    inverse = 1.0 / counts[0:1]

    def remote(src, dst, ssem, rsem, peer):
        return pltpu.make_async_remote_copy(
            src_ref=src, dst_ref=dst, send_sem=ssem, recv_sem=rsem,
            device_id={"tm": peer}, device_id_type=MESH,
        )

    def first_part(i, o):
        at = pl.ds(i * vb, vb)
        dest = lax.rem(c + o, slab)
        return remote(
            send.at[0, dest, :, :, at, :], recv_a.at[0, c, :, :, at, :],
            a0s.at[i, o], a0r.at[i, o], in_slab(o),
        )

    def first(s, o):
        dest = lax.rem(c + o, slab)
        return remote(send.at[s, dest], recv_a.at[s, c], as_.at[s, o], ar.at[s, o], in_slab(o))

    def second(s, o):
        dest = lax.rem(z + o, RADIX)
        return remote(send_b.at[s, dest], recv_b.at[s, z], bs.at[s, o], br.at[s, o], across(o))

    def third(s, o):
        dest = lax.rem(c + o, slab)
        return remote(send.at[s, dest], recv_c.at[s, c], cs.at[s, o], cr.at[s, o], in_slab(o))

    for i in range(BLOCKS):
        for r in range(RADIX):
            load(i, r).wait()
        high, low = split_bf16(vis_buf[i].reshape(tb * width, vis_buf.shape[-1]))
        summed = lax.dot_general(high, wt[...], NT, preferred_element_type=jnp.float32)
        summed += lax.dot_general(low, wt[...], NT, preferred_element_type=jnp.float32)
        mean = summed * inverse
        for j in range(tiles):
            avg[j] = mean[:, j * LANES:(j + 1) * LANES]
        for j in range(tiles):
            for f in range(chans):
                for r in range(RADIX):
                    for p in range(2):
                        send[j * per_dev + f % per_dev, f // per_dev, r, p, i * vb:(i + 1) * vb, :] = avg[
                            j, pl.ds(r * vb * width + p * chans + f, vb, stride=width), :
                        ]
        if i == 0:
            pl.semaphore_wait(barrier, len(peers))
        for o in range(1, slab):
            first_part(i, o).start()
    for s in range(1, steps):
        for o in range(1, slab):
            first(s, o).start()
    for j in range(2):
        fetch(j, j).start()

    def keep(s, carry):
        recv_a[s, c] = send[s, c]
        return carry

    lax.fori_loop(0, steps, keep, 0)
    part[...] = jnp.zeros_like(part)
    for copy in table_copies:
        copy.wait()

    def encode(s):
        for r in range(RADIX):
            x = recv_a[s, :, r].reshape(slab * 2 * per, LANES)
            mix[r] = stacked_dot(enc[r], x)[:mix.shape[1]]

        def put(k, at, v):
            send_b[s, k, at, :] = v

        dft_radix(lambda k, at: mix[k, at, :], put, rank)
        recv_b[s, z] = send_b[s, z]
        for o in range(1, RADIX):
            second(s, o).start()

    def decode(s):
        for o in range(1, RADIX):
            second(s, o).wait_recv()

        def put(k, at, v):
            back[k, at, :] = v

        dft_radix(lambda k, at: recv_b[s, k, at, :], put, rank)
        for r in range(RADIX):
            y = stacked_dot(dec[r], back[r]).reshape(slab, 2, per, LANES)
            for d in range(slab):
                send[s, d, r] = y[d]
        recv_c[s, c] = send[s, c]
        for o in range(1, slab):
            third(s, o).start()

    def place(s, j, f2):
        for o in range(1, slab):
            third(s, o).wait_recv()

        def one(d, carry):
            for r in range(RADIX):
                for p in range(2):
                    start = (r * 2 + p) * chans + f2 + d * per_dev
                    lay[j, pl.ds(start, per, stride=RADIX * width), :] = recv_c[s, d, r, p]
            return carry

        lax.fori_loop(0, slab, one, 0)

    def write(j):
        return pltpu.make_async_copy(
            lay.at[j], mm_ref.at[:, pl.ds(pl.multiple_of(j * LANES, LANES), LANES)], out_sem.at[j]
        )

    def project(j, slot, m):
        at = pl.multiple_of(m * width, width)
        x0 = rounded(lay[j, pl.ds(at, chans), :])
        x1 = rounded(lay[j, pl.ds(at + chans, chans), :])
        f0 = filt[slot, m, 0].astype(jnp.float32)
        f1 = filt[slot, m, 1].astype(jnp.float32)
        part[m, 0] += jnp.sum(f0 * x0 - f1 * x1, axis=1)
        part[m, 1] += jnp.sum(f0 * x1 + f1 * x0, axis=1)

    def finish(j):
        for f2 in range(per_dev):
            place(j * per_dev + f2, j, f2)
        write(j).start()
        slot = lax.rem(j, 2)
        fetch(j, slot).wait()

        def one(m, carry):
            project(j, slot, m)
            return carry

        lax.fori_loop(0, local, one, 0)

        @pl.when(j + 2 < tiles)
        def _():
            fetch(j + 2, slot).start()

    back[:, total:, :] = jnp.zeros((RADIX, back.shape[1] - total, LANES), jnp.float32)
    for i in range(BLOCKS):
        for o in range(1, slab):
            first_part(i, o).wait_recv()
    encode(0)
    for i in range(BLOCKS):
        for o in range(1, slab):
            first_part(i, o).wait_send()

    def step(d, carry):
        for q in (1, 2):
            e = 2 * d + q

            @pl.when(e < steps)
            def _():
                for o in range(1, slab):
                    first(e, o).wait_recv()
                encode(e)

        @pl.when((d >= per_dev + 1) & (lax.rem(d, per_dev) == per_dev - 1))
        def _():
            finish(lax.div(d - per_dev - 1, per_dev))

        @pl.when(d > 0)
        def _():
            for o in range(1, slab):
                first(d, o).wait_send()

        decode(d)
        return carry

    lax.fori_loop(0, steps, step, 0)

    j = tiles - 1
    for f2 in range(per_dev):
        place(j * per_dev + f2, j, f2)
    write(j).start()
    fetch(j, j % 2).wait()
    group = modes_ref.shape[2] // (2 * kept)

    def last(k, carry):
        def one(m, inner):
            project(j, j % 2, k * group + m)
            return inner

        lax.fori_loop(0, group, one, 0)
        sums = part[pl.ds(k * group, group)].reshape(group * 2 * kept, LANES)
        high, low = split_bf16(sums)
        whole = lax.dot_general(
            jnp.ones((8, 2 * LANES), jnp.bfloat16), jnp.concatenate([high, low], axis=1), NT,
            preferred_element_type=jnp.float32,
        )
        modes_ref[k] = whole[0:1]
        return carry

    lax.fori_loop(0, modes_ref.shape[0], last, 0)

    def drain(s, carry):
        for o in range(1, RADIX):
            second(s, o).wait_send()
        for o in range(1, slab):
            third(s, o).wait_send()
        return carry

    lax.fori_loop(0, steps, drain, 0)
    for t in range(tiles):
        write(t).wait()


def fits(n, local, chans, raw, uniq, kept):
    slab = n // RADIX
    return (
        n == RADIX * slab
        and slab > 1
        and chans == 8
        and chans % slab == 0
        and local % (BLOCKS * RADIX * 8) == 0
        and slab * local * 2 // RADIX <= 2 * LANES
        and raw % LANES == 0
        and raw <= 8 * LANES
        and uniq % LANES == 0
        and 2 * LANES <= uniq <= 4 * LANES
        and kept == 16
        and chans // slab == 2
    )


def fused_device(visibilities, redundancy, mode_counts, filters):
    n = lax.axis_size("tm")
    local, _, chans, raw = visibilities.shape
    uniq, kept = filters.shape[4], filters.shape[2]
    slab = n // RADIX
    tiles = uniq // LANES
    per_dev = chans // slab
    steps = tiles * per_dev
    per = local // RADIX
    width = 2 * chans
    tb = local // BLOCKS
    rank, enc, dec = stacked_tables(slab, local)
    total = 2 * rank
    vmem = pl.BlockSpec(memory_space=pltpu.VMEM)
    hbm = pl.BlockSpec(memory_space=pl.ANY)
    f32, bf16 = jnp.float32, jnp.bfloat16
    dma = pltpu.SemaphoreType.DMA
    group = 16
    mmodes, flat = pl.pallas_call(
        functools.partial(fused_kernel, n, local, chans, uniq, kept, rank),
        out_shape=(
            jax.ShapeDtypeStruct((local * width, uniq), f32),
            jax.ShapeDtypeStruct((local // group, 1, group * 2 * kept), f32),
        ),
        in_specs=[hbm] * 4 + [vmem],
        out_specs=(hbm, vmem),
        scratch_shapes=[
            pltpu.VMEM((BLOCKS, RADIX, tb // RADIX, width, raw), f32),
            pltpu.VMEM((uniq, raw), bf16),
            pltpu.VMEM((tiles, tb * width, LANES), f32),
            pltpu.VMEM((steps, slab, RADIX, 2, per, LANES), f32),
            pltpu.VMEM((steps, slab, RADIX, 2, per, LANES), f32),
            pltpu.VMEM((RADIX, total, LANES), f32),
            pltpu.VMEM((steps, RADIX, total, LANES), f32),
            pltpu.VMEM((steps, RADIX, total, LANES), f32),
            pltpu.VMEM((RADIX, dec.shape[2], LANES), f32),
            pltpu.VMEM((steps, slab, RADIX, 2, per, LANES), f32),
            pltpu.VMEM((tiles, local * width, LANES), f32),
            pltpu.VMEM((local, 2, kept, LANES), f32),
            pltpu.VMEM((2, local, 2, kept, chans, LANES), bf16),
            pltpu.VMEM(enc.shape, bf16),
            pltpu.VMEM(dec.shape, bf16),
            dma((BLOCKS, RADIX)),
            dma((2,)),
            dma((BLOCKS, slab)),
            dma((BLOCKS, slab)),
            dma((steps, slab)),
            dma((steps, slab)),
            dma((steps, RADIX)),
            dma((steps, RADIX)),
            dma((steps, slab)),
            dma((steps, slab)),
            dma((2,)),
            dma((tiles,)),
        ],
        compiler_params=pltpu.CompilerParams(
            collective_id=0, has_side_effects=True, vmem_limit_bytes=67043328 - 2**17
        ),
        name="fused",
    )(
        visibilities.reshape(local // RADIX, RADIX, width, raw),
        filters, enc, dec, redundancy.reshape(1, raw),
    )
    coefs = flat.reshape(local, 2, kept)
    kept_mask = lax.broadcasted_iota(jnp.int32, (local, kept), 1) < mode_counts[:, None]
    return mmodes.reshape(local, 2, chans, uniq), jnp.where(kept_mask[:, None, :], coefs, 0.0)


def phase_table(numer, period):
    phases = 2.0 * jnp.pi / period * numer.astype(jnp.float32)
    return (jnp.cos(phases), jnp.sin(phases))


def apply_stacked(cosine, sine_table, stacked, width):
    cos_part = jnp.dot(
        cosine, stacked, precision=lax.Precision.HIGHEST, preferred_element_type=jnp.float32
    )
    sin_part = jnp.dot(
        sine_table, stacked, precision=lax.Precision.HIGHEST, preferred_element_type=jnp.float32
    )
    real_out = cos_part[:, :width] + sin_part[:, width:]
    imag_out = cos_part[:, width:] - sin_part[:, :width]
    return jnp.concatenate([real_out, imag_out], axis=1)


def factored_transform(stacked, width):
    length = stacked.shape[0]
    radix_size = 64
    inner_size = length // radix_size
    outer_row = lax.broadcasted_iota(jnp.int32, (radix_size, radix_size), 0)
    outer_col = lax.broadcasted_iota(jnp.int32, (radix_size, radix_size), 1)
    cosine, sine_table = phase_table(outer_row * outer_col % radix_size, radix_size)
    grouped = stacked.reshape(radix_size, inner_size, 2, width)
    grouped = jnp.transpose(grouped, (0, 2, 1, 3)).reshape(radix_size, 2 * inner_size * width)
    section = apply_stacked(cosine, sine_table, grouped, inner_size * width)
    section = section.reshape(radix_size, 2, inner_size, width)
    section_real = section[:, 0]
    section_imag = section[:, 1]
    twist_row = lax.broadcasted_iota(jnp.int32, (radix_size, inner_size, 1), 0)
    twist_col = lax.broadcasted_iota(jnp.int32, (radix_size, inner_size, 1), 1)
    twist_cos, twist_sin = phase_table(twist_row * twist_col, length)
    turned_real = section_real * twist_cos + section_imag * twist_sin
    turned_imag = section_imag * twist_cos - section_real * twist_sin
    turned = jnp.stack([turned_real, turned_imag], axis=0)
    turned = jnp.transpose(turned, (2, 0, 1, 3)).reshape(inner_size, 2 * radix_size * width)
    inner_row = lax.broadcasted_iota(jnp.int32, (inner_size, inner_size), 0)
    inner_col = lax.broadcasted_iota(jnp.int32, (inner_size, inner_size), 1)
    cosine2, sine_table2 = phase_table(inner_row * inner_col % inner_size, inner_size)
    final = apply_stacked(cosine2, sine_table2, turned, radix_size * width)
    final = final.reshape(inner_size, 2, radix_size, width)
    return jnp.transpose(final, (0, 2, 1, 3)).reshape(length, 2 * width)


def transform(columns):
    length, _, width = columns.shape
    stacked = columns.reshape(length, 2 * width)
    result = factored_transform(stacked, width)
    scale = 1.0 / jnp.sqrt(jnp.float32(length))
    return (result * scale).reshape(length, 2, width)


def on_device(visibilities, redundancy, mode_counts, filters):
    groups = lax.axis_size("tm")
    local_times, _, channels, raw_count = visibilities.shape
    uniques = filters.shape[4]
    kept = filters.shape[2]
    if fits(groups, local_times, channels, raw_count, uniques, kept):
        return fused_device(visibilities, redundancy, mode_counts, filters)
    unique_block = uniques // groups
    members = (
        redundancy[:, None] == lax.broadcasted_iota(jnp.int32, (raw_count, uniques), 1)
    ).astype(jnp.float32)
    weights = members / jnp.sum(members, axis=0, keepdims=True)
    flat_rows = visibilities.reshape(local_times, 2 * channels, raw_count)
    blocked_weights = weights.reshape(raw_count, groups, unique_block)
    packed = jnp.einsum(
        "tqr,rjc->tjqc",
        flat_rows,
        blocked_weights,
        precision=lax.Precision.HIGHEST,
        preferred_element_type=jnp.float32,
    )
    packed = packed.reshape(local_times, groups, 2 * channels * unique_block)
    arrived = lax.all_to_all(packed, "tm", split_axis=1, concat_axis=0, tiled=True)
    length = arrived.shape[0]
    spectra = transform(arrived.reshape(length, 2, channels * unique_block))
    spectra = spectra.reshape(length, 1, 2 * channels * unique_block)
    regrouped = lax.all_to_all(spectra, "tm", split_axis=0, concat_axis=1, tiled=True)
    regrouped = regrouped.reshape(local_times, groups, 2, channels, unique_block)
    mmodes = jnp.transpose(regrouped, (0, 2, 3, 1, 4)).reshape(local_times, 2, channels, uniques)
    local_modes = mmodes.shape[0]
    rounded = mmodes.astype(jnp.bfloat16).reshape(local_modes, 2, channels * uniques)
    flat_filters = filters.reshape(local_modes, 2, kept, channels * uniques)
    products = jnp.einsum(
        "mpkc,mqc->mpqk", flat_filters, rounded, preferred_element_type=jnp.float32
    )
    real_out = products[:, 0, 0] - products[:, 1, 1]
    imag_out = products[:, 0, 1] + products[:, 1, 0]
    kept_mask = lax.broadcasted_iota(jnp.int32, (local_modes, kept), 1) < mode_counts[:, None]
    modes = jnp.where(kept_mask[:, None, :], jnp.stack([real_out, imag_out], axis=1), 0.0)
    return (mmodes, modes)


def solution(mesh):
    return jax.shard_map(
        on_device,
        mesh=mesh,
        in_specs=(P("tm", None, "grp", None), P("grp"), P("tm"), P("tm", None, None, "grp", None)),
        out_specs=(P("tm", None, "grp", None), P("tm", None, "grp")),
        check_vma=False,
    )
```

time: 212 us -> 152 us (0.72)
  Pallas kernels: 209 us -> 143 us
  local copies, waits for them, and re-layouts: 0.9 us -> 5.94 us
    pallas_call x2 -> x1, Pallas kernels: 209 us -> 143 us  [fused_device(): pl.pallas_call(functools.partial(fused_kernel, n, local, chans, uniq, kep...]
    unnamed x3 -> x4, local copies, waits for them, and re-layouts: 0.69 us -> 5.73 us
where the time goes in v1:
time: 152 us; the launch traced here: 150 us
  Pallas kernels  143 us (94%)
  local copies, waits for them, and re-layouts  5.94 us (4%)
    pallas_call x1, Pallas kernels, fused_device(): pl.pallas_call(functools.partial(fused_kernel, n, local, chans, uniq, kep...  143 us
    unnamed x4, local copies, waits for them, and re-layouts  5.73 us

profile of v1, /device:TPU:13, one launch (start us, length us, event | category | flops | bytes accessed | tf_op | source)
XLA Modules:
  0.0 150.4 jit_solution(3829901817447259900)
XLA Ops:
  0.6 0.0 copy-start
  0.6 142.9 %fused.1 = (f32[2048,512]{1,0:T(8,128)}, f32[8,1,512]{2,1,0:T(1,128)}) custom-call(f32[32,4,16,1024]{3,2,1,0:T(8,128)} %bitcast.3, bf16[128,2,16,8,512]{4,3,2,1,0:T(8,128)(2,1)} %filt_ref.1, bf16[4,608,256]{2,1,0:T(8,128)(2,1)} %constant.6.clone.enc_hbm, bf16[4,512,384]{2,1,0:T(8,128)(2,1)} %constant.7.clone.dec_hbm, s32[1,1024]{1,0:T(1,128)} %bitcast.5), custom_call_target="tpu_custom_call" | custom-call | tf_op jit(solution)/shard_map/fused/pallas_call | solution.py:423
  143.5 0.8 reduce
  144.3 0.2 reshape.34
  144.5 0.0 copy-done
  144.5 0.1 iota_compare_fusion
  144.6 0.1 broadcast_select_fusion
  144.7 0.7 copy.9
  145.4 5.0 %copy.11 = f32[128,2,8,512]{3,2,1,0:T(8,128)} copy(f32[128,2,8,512]{3,2,1,0:T(8,128)} %bitcast.4) | data formatting | bytes 8388608
Async XLA Ops:
  0.6 143.9 %copy-start = (s32[128]{0:T(128)S(1)}, s32[128]{0:T(128)}, u32[]{:S(2)}) copy-start(s32[128]{0:T(128)} %param.8) | copy-start | bytes 1540

commit v2 on v1

--- a/solution.py
+++ b/solution.py
@@ -12,6 +12,8 @@
 LANES = 128
 BLOCKS = 4
 RADIX = 4
+AHEAD = 3
+SLOTS = 3
 NT = (((1,), (1,)), ((), ()))
 
 
@@ -125,9 +127,9 @@
 
 def fused_kernel(
     n, local, chans, uniq, kept, rank,
-    vis_ref, filt_ref, enc_hbm, dec_hbm, red_ref, mm_ref, modes_ref,
-    vis_buf, wt, avg, send, recv_a, mix, send_b, recv_b, back, recv_c, lay, part, filt, enc, dec,
-    load_sem, tab_sem, a0s, a0r, as_, ar, bs, br, cs, cr, filt_sem, out_sem,
+    vis_ref, filt_ref, enc_hbm, dec_hbm, red_ref, counts_ref, mm_ref, modes_ref,
+    send, recv_a, mix, send_b, recv_b, back, recv_c, part, turned, enc, dec,
+    load_sem, tab_sem, as_, ar, bs, br, cs, cr, filt_sem,
 ):
     slab = n // RADIX
     me = lax.axis_index("tm")
@@ -141,28 +143,10 @@
     width = 2 * chans
     total = 2 * rank
 
-    def load(i, r):
-        return pltpu.make_async_copy(
-            vis_ref.at[pl.ds(i * vb, vb), r], vis_buf.at[i, r], load_sem.at[i, r]
-        )
-
-    def fetch(j, slot):
-        return pltpu.make_async_copy(
-            filt_ref.at[:, :, :, :, pl.ds(pl.multiple_of(j * LANES, LANES), LANES)],
-            filt.at[slot],
-            filt_sem.at[slot],
-        )
-
     table_copies = [
         pltpu.make_async_copy(enc_hbm, enc, tab_sem.at[0]),
         pltpu.make_async_copy(dec_hbm, dec, tab_sem.at[1]),
     ]
-    for i in range(BLOCKS):
-        for r in range(RADIX):
-            load(i, r).start()
-    for copy in table_copies:
-        copy.start()
-
     def in_slab(o):
         return z * slab + lax.rem(c + o, slab)
 
@@ -171,16 +155,6 @@
 
     barrier = pltpu.get_barrier_semaphore()
     peers = [in_slab(o) for o in range(1, slab)] + [across(o) for o in range(1, RADIX)]
-    for peer in peers:
-        pl.semaphore_signal(barrier, inc=1, device_id={"tm": peer}, device_id_type=MESH)
-
-    wt[...] = (
-        lax.broadcasted_iota(jnp.int32, wt.shape, 0) == red_ref[...]
-    ).astype(jnp.float32).astype(jnp.bfloat16)
-    ones = jnp.ones((8, wt.shape[1]), jnp.bfloat16)
-    counts = lax.dot_general(ones, wt[...], NT, preferred_element_type=jnp.float32)
-    inverse = 1.0 / counts[0:1]
-
     def remote(src, dst, ssem, rsem, peer):
         return pltpu.make_async_remote_copy(
             src_ref=src, dst_ref=dst, send_sem=ssem, recv_sem=rsem,
@@ -188,59 +162,36 @@
         )
 
     def first_part(i, o):
-        at = pl.ds(i * vb, vb)
+        at = pl.ds(i * vb if isinstance(i, int) else pl.multiple_of(i * vb, vb), vb)
         dest = lax.rem(c + o, slab)
         return remote(
             send.at[0, dest, :, :, at, :], recv_a.at[0, c, :, :, at, :],
-            a0s.at[i, o], a0r.at[i, o], in_slab(o),
+            as_.at[0], ar.at[0], in_slab(o),
         )
 
     def first(s, o):
         dest = lax.rem(c + o, slab)
-        return remote(send.at[s, dest], recv_a.at[s, c], as_.at[s, o], ar.at[s, o], in_slab(o))
+        return remote(send.at[s, dest], recv_a.at[s, c], as_.at[s], ar.at[s], in_slab(o))
 
     def second(s, o):
         dest = lax.rem(z + o, RADIX)
-        return remote(send_b.at[s, dest], recv_b.at[s, z], bs.at[s, o], br.at[s, o], across(o))
+        return remote(send_b.at[s, dest], recv_b.at[s, z], bs, br.at[s], across(o))
+
+    def all_first(s):
+        some = pl.ds(0, slab - 1)
+        return remote(send.at[s, some], recv_a.at[s, some], as_.at[s], ar.at[s], in_slab(1))
+
+    def all_second(s):
+        some = pl.ds(0, RADIX - 1)
+        return remote(send_b.at[s, some], recv_b.at[s, some], bs, br.at[s], across(1))
+
+    def all_third(s):
+        some = pl.ds(0, slab - 1)
+        return remote(send.at[s, some], recv_c.at[s, some], cs, cr.at[s], in_slab(1))
 
     def third(s, o):
         dest = lax.rem(c + o, slab)
-        return remote(send.at[s, dest], recv_c.at[s, c], cs.at[s, o], cr.at[s, o], in_slab(o))
-
-    for i in range(BLOCKS):
-        for r in range(RADIX):
-            load(i, r).wait()
-        high, low = split_bf16(vis_buf[i].reshape(tb * width, vis_buf.shape[-1]))
-        summed = lax.dot_general(high, wt[...], NT, preferred_element_type=jnp.float32)
-        summed += lax.dot_general(low, wt[...], NT, preferred_element_type=jnp.float32)
-        mean = summed * inverse
-        for j in range(tiles):
-            avg[j] = mean[:, j * LANES:(j + 1) * LANES]
-        for j in range(tiles):
-            for f in range(chans):
-                for r in range(RADIX):
-                    for p in range(2):
-                        send[j * per_dev + f % per_dev, f // per_dev, r, p, i * vb:(i + 1) * vb, :] = avg[
-                            j, pl.ds(r * vb * width + p * chans + f, vb, stride=width), :
-                        ]
-        if i == 0:
-            pl.semaphore_wait(barrier, len(peers))
-        for o in range(1, slab):
-            first_part(i, o).start()
-    for s in range(1, steps):
-        for o in range(1, slab):
-            first(s, o).start()
-    for j in range(2):
-        fetch(j, j).start()
-
-    def keep(s, carry):
-        recv_a[s, c] = send[s, c]
-        return carry
-
-    lax.fori_loop(0, steps, keep, 0)
-    part[...] = jnp.zeros_like(part)
-    for copy in table_copies:
-        copy.wait()
+        return remote(send.at[s, dest], recv_c.at[s, c], cs, cr.at[s], in_slab(o))
 
     def encode(s):
         for r in range(RADIX):
@@ -255,9 +206,132 @@
         for o in range(1, RADIX):
             second(s, o).start()
 
+    odd = lax.rem(c, 2)
+    near, ahead, behind = 1 + 2 * odd, 2 - odd, 3 - odd
+
+    def averages(vis_buf, wt, avg):
+        def load(i, r):
+            return pltpu.make_async_copy(
+                vis_ref.at[pl.ds(i * vb, vb), r], vis_buf.at[i, r], load_sem.at[i]
+            )
+
+        for i in range(2):
+            for r in range(RADIX):
+                load(i, r).start()
+        for peer in peers:
+            pl.semaphore_signal(barrier, inc=1, device_id={"tm": peer}, device_id_type=MESH)
+        wt[...] = (
+            lax.broadcasted_iota(jnp.int32, wt.shape, 0) == red_ref[...]
+        ).astype(jnp.float32).astype(jnp.bfloat16)
+        ones = jnp.ones((8, wt.shape[1]), jnp.bfloat16)
+        for i in range(2, BLOCKS):
+            for r in range(RADIX):
+                load(i, r).start()
+        for copy in table_copies:
+            copy.start()
+        counts = lax.dot_general(ones, wt[...], NT, preferred_element_type=jnp.float32)
+        inverse = 1.0 / counts[0:1]
+
+        def average(i, h):
+            at = pl.ds(i * vb if isinstance(i, int) else pl.multiple_of(i * vb, vb), vb)
+            high, low = split_bf16(vis_buf[i].reshape(tb * width, vis_buf.shape[-1]))
+            lanes = slice(h * 2 * LANES, (h + 1) * 2 * LANES)
+            members = wt[lanes, :]
+            summed = lax.dot_general(high, members, NT, preferred_element_type=jnp.float32)
+            summed += lax.dot_general(low, members, NT, preferred_element_type=jnp.float32)
+            mean = summed * inverse[:, lanes]
+            for q in range(2):
+                avg[q] = mean[:, q * LANES:(q + 1) * LANES]
+            for q in range(2):
+                for f in range(chans):
+                    for r in range(RADIX):
+                        for p in range(2):
+                            s = (h * 2 + q) * per_dev + f % per_dev
+                            send[s, f // per_dev, r, p, at, :] = avg[
+                                q, pl.ds(r * vb * width + p * chans + f, vb, stride=width), :
+                            ]
+
+        def early(i, carry):
+            pltpu.make_async_copy(vis_buf.at[i], vis_buf.at[i], load_sem.at[i]).wait()
+            average(i, 0)
+
+            @pl.when(i == 0)
+            def _():
+                pl.semaphore_wait(barrier, len(peers))
+
+            first_part(i, near).start()
+            first_part(i, ahead).start()
+            return carry
+
+        lax.fori_loop(0, BLOCKS, early, 0)
+        for i in range(BLOCKS):
+            first_part(i, behind).start()
+        recv_a[0, c] = send[0, c]
+        for copy in table_copies:
+            copy.wait()
+        all_first(0).wait_recv()
+        for s in (1, 2):
+            for o in range(1, slab):
+                first(s, o).start()
+        encode(0)
+
+        def more(i, carry):
+            average(i, 1)
+            return carry
+
+        lax.fori_loop(0, BLOCKS, more, 0)
+
+    pl.run_scoped(
+        averages,
+        pltpu.VMEM((BLOCKS, RADIX, tb // RADIX, width, vis_ref.shape[-1]), jnp.float32),
+        pltpu.VMEM((uniq, vis_ref.shape[-1]), jnp.bfloat16),
+        pltpu.VMEM((2, tb * width, LANES), jnp.float32),
+    )
+
+    pl.run_scoped(
+        functools.partial(
+            transform_kernel, n, local, chans, uniq, kept, rank, filt_ref, counts_ref, mm_ref, modes_ref,
+            send, recv_a, mix, send_b, recv_b, back, recv_c, part, turned, enc, dec,
+            first, second, third, all_first, all_second, all_third, encode, filt_sem,
+        ),
+        pltpu.VMEM((SLOTS, local, 2, kept, chans, LANES), jnp.bfloat16),
+    )
+
+
+def transform_kernel(
+    n, local, chans, uniq, kept, rank, filt_ref, counts_ref, mm_ref, modes_ref,
+    send, recv_a, mix, send_b, recv_b, back, recv_c, part, turned, enc, dec,
+    first, second, third, all_first, all_second, all_third, encode, filt_sem, filt,
+):
+    slab = n // RADIX
+    me = lax.axis_index("tm")
+    z, c = lax.div(me, slab), lax.rem(me, slab)
+    tiles = uniq // LANES
+    per_dev = chans // slab
+    steps = tiles * per_dev
+    per = local // RADIX
+    width = 2 * chans
+    total = 2 * rank
+    stride = part.shape[0] // local
+
+    def fetch(j):
+        at = pl.multiple_of(j * LANES, LANES)
+        slot = lax.rem(j, SLOTS)
+        return pltpu.make_async_copy(
+            filt_ref.at[:, :, :, :, pl.ds(at, LANES)], filt.at[slot], filt_sem.at[slot]
+        )
+
+    for j in range(SLOTS):
+        fetch(j).start()
+
+    def keep(s, carry):
+        recv_a[s, c] = send[s, c]
+        return carry
+
+    lax.fori_loop(1, steps, keep, 0)
+    part[...] = jnp.zeros_like(part)
     def decode(s):
-        for o in range(1, RADIX):
-            second(s, o).wait_recv()
+        all_second(s).wait_recv()
 
         def put(k, at, v):
             back[k, at, :] = v
@@ -272,123 +346,166 @@
             third(s, o).start()
 
     def place(s, j, f2):
-        for o in range(1, slab):
-            third(s, o).wait_recv()
+        all_third(s).wait_recv()
 
         def one(d, carry):
             for r in range(RADIX):
                 for p in range(2):
                     start = (r * 2 + p) * chans + f2 + d * per_dev
-                    lay[j, pl.ds(start, per, stride=RADIX * width), :] = recv_c[s, d, r, p]
+                    mm_ref[j, pl.ds(start, per, stride=RADIX * width), :] = recv_c[s, d, r, p]
             return carry
 
         lax.fori_loop(0, slab, one, 0)
 
-    def write(j):
-        return pltpu.make_async_copy(
-            lay.at[j], mm_ref.at[:, pl.ds(pl.multiple_of(j * LANES, LANES), LANES)], out_sem.at[j]
-        )
-
-    def project(j, slot, m):
-        at = pl.multiple_of(m * width, width)
-        x0 = rounded(lay[j, pl.ds(at, chans), :])
-        x1 = rounded(lay[j, pl.ds(at + chans, chans), :])
-        f0 = filt[slot, m, 0].astype(jnp.float32)
-        f1 = filt[slot, m, 1].astype(jnp.float32)
-        part[m, 0] += jnp.sum(f0 * x0 - f1 * x1, axis=1)
-        part[m, 1] += jnp.sum(f0 * x1 + f1 * x0, axis=1)
-
-    def finish(j):
-        for f2 in range(per_dev):
-            place(j * per_dev + f2, j, f2)
-        write(j).start()
-        slot = lax.rem(j, 2)
-        fetch(j, slot).wait()
+    def turn(j):
+        slot = lax.rem(j, SLOTS)
+        fetch(j).wait()
 
         def one(m, carry):
-            project(j, slot, m)
+            for p in range(2):
+                turned[p] = filt[slot, m, p].astype(jnp.float32).reshape(kept * chans, LANES)
+            for p in range(2):
+                for f in range(chans):
+                    for g in range(kept // 8):
+                        rows = turned[p, pl.ds(g * 8 * chans + f, 8, stride=chans), :]
+                        filt[slot, m, p, f * (kept // 8) + g] = rows.astype(jnp.bfloat16)
             return carry
 
         lax.fori_loop(0, local, one, 0)
 
-        @pl.when(j + 2 < tiles)
-        def _():
-            fetch(j + 2, slot).start()
+    def project(j, f2, m):
+        slot = lax.rem(j, SLOTS)
+        per_chan = kept // 8
+        re = pl.ds(pl.multiple_of(m * stride, 8), kept)
+        im = pl.ds(pl.multiple_of(m * stride + kept, 8), kept)
+        real, imag = part[re, :], part[im, :]
+        for d in range(slab):
+            f = d * per_dev + f2
+            at = f * per_chan
+            x0 = mm_ref[j, pl.ds(m * width + f, 1), :].astype(jnp.bfloat16).astype(jnp.float32)
+            x1 = mm_ref[j, pl.ds(m * width + chans + f, 1), :].astype(jnp.bfloat16).astype(jnp.float32)
+            f0 = filt[slot, m, 0, pl.ds(at, per_chan)].astype(jnp.float32).reshape(kept, LANES)
+            f1 = filt[slot, m, 1, pl.ds(at, per_chan)].astype(jnp.float32).reshape(kept, LANES)
+            real += f0 * x0 - f1 * x1
+            imag += f0 * x1 + f1 * x0
+        part[re, :] = real
+        part[im, :] = imag
+
+    def projects(j, f2, low, high):
+        def one(m, carry):
+            project(j, f2, m)
+            return carry
+
+        lax.fori_loop(low, high, one, 0, unroll=2)
 
     back[:, total:, :] = jnp.zeros((RADIX, back.shape[1] - total, LANES), jnp.float32)
-    for i in range(BLOCKS):
-        for o in range(1, slab):
-            first_part(i, o).wait_recv()
-    encode(0)
-    for i in range(BLOCKS):
-        for o in range(1, slab):
-            first_part(i, o).wait_send()
-
-    def step(d, carry):
-        for q in (1, 2):
-            e = 2 * d + q
-
-            @pl.when(e < steps)
-            def _():
-                for o in range(1, slab):
-                    first(e, o).wait_recv()
-                encode(e)
-
-        @pl.when((d >= per_dev + 1) & (lax.rem(d, per_dev) == per_dev - 1))
-        def _():
-            finish(lax.div(d - per_dev - 1, per_dev))
-
-        @pl.when(d > 0)
+
+    def later(e):
+        all_first(e).wait_recv()
+
+        @pl.when(e + 2 < steps)
         def _():
             for o in range(1, slab):
-                first(d, o).wait_send()
-
+                first(e + 2, o).start()
+
+        encode(e)
+
+    for e in range(1, AHEAD):
+        later(e)
+
+    def step(d, carry):
+        @pl.when(d < SLOTS)
+        def _():
+            turn(d)
+
+        @pl.when(d >= 2)
+        def _():
+            j, f2 = lax.div(d - 2, per_dev), lax.rem(d - 2, per_dev)
+            place(d - 2, j, f2)
+
+            projects(j, f2, 0, local)
+
+            @pl.when((f2 == per_dev - 1) & (j + SLOTS < tiles))
+            def _():
+                fetch(j + SLOTS).start()
+
+        @pl.when((d >= steps - 2) & (d - (steps - 2) + SLOTS < tiles))
+        def _():
+            turn(d - (steps - 2) + SLOTS)
+
+        all_first(d).wait_send()
         decode(d)
+
+        @pl.when(d + AHEAD < steps)
+        def _():
+            later(d + AHEAD)
+
         return carry
 
     lax.fori_loop(0, steps, step, 0)
 
     j = tiles - 1
+    lane = lax.broadcasted_iota(jnp.int32, (kept, LANES), 1)
+
+    def gather(q, outs):
+        outs = list(outs)
+        for i in range(8):
+            m = q * 8 + i
+            for p in range(2):
+                at = pl.ds(pl.multiple_of(m * stride + p * kept, 8), kept)
+                row = jnp.sum(part[at, :], axis=1, keepdims=True)
+                outs[p] = jnp.where(lane == m, row, outs[p])
+        return tuple(outs)
+
+    def last(q, outs):
+        outs = gather(jnp.maximum(q - 1, 0), outs)
+        for i in range(8):
+            project(j, per_dev - 1, q * 8 + i)
+        return outs
+
     for f2 in range(per_dev):
         place(j * per_dev + f2, j, f2)
-    write(j).start()
-    fetch(j, j % 2).wait()
-    group = modes_ref.shape[2] // (2 * kept)
-
-    def last(k, carry):
-        def one(m, inner):
-            project(j, j % 2, k * group + m)
-            return inner
-
-        lax.fori_loop(0, group, one, 0)
-        sums = part[pl.ds(k * group, group)].reshape(group * 2 * kept, LANES)
-        high, low = split_bf16(sums)
-        whole = lax.dot_general(
-            jnp.ones((8, 2 * LANES), jnp.bfloat16), jnp.concatenate([high, low], axis=1), NT,
-            preferred_element_type=jnp.float32,
+        if f2 < per_dev - 1:
+            projects(j, f2, 0, local)
+    zero = jnp.zeros((kept, LANES), jnp.float32)
+    outs = lax.fori_loop(0, local // 8, last, (zero, zero))
+    outs = gather(local // 8 - 1, outs)
+    order = lax.broadcasted_iota(jnp.int32, (kept, LANES), 0)
+    for p in range(2):
+        modes_ref[p] = jnp.where(order < counts_ref[...], outs[p], 0.0)
+
+    def drain(s, carry):
+        all_second(s).wait_send()
+        all_third(s).wait_send()
+        return carry
+
+    lax.fori_loop(0, steps, drain, 0)
+
+
+def emit_kernel(mm_ref, modes_ref, out_ref, kept_ref, out_sem):
+    tiles, chunks = out_sem.shape
+    rows = mm_ref.shape[1] // chunks
+
+    def write(t, q):
+        at = pl.ds(q * rows, rows)
+        return pltpu.make_async_copy(
+            mm_ref.at[t, at], out_ref.at[at, pl.ds(t * LANES, LANES)], out_sem.at[t, q]
         )
-        modes_ref[k] = whole[0:1]
-        return carry
-
-    lax.fori_loop(0, modes_ref.shape[0], last, 0)
-
-    def drain(s, carry):
-        for o in range(1, RADIX):
-            second(s, o).wait_send()
-        for o in range(1, slab):
-            third(s, o).wait_send()
-        return carry
-
-    lax.fori_loop(0, steps, drain, 0)
+
     for t in range(tiles):
-        write(t).wait()
+        for q in range(chunks):
+            write(t, q).start()
+    kept_ref[...] = modes_ref[...]
+    for t in range(tiles):
+        for q in range(chunks):
+            write(t, q).wait()
 
 
 def fits(n, local, chans, raw, uniq, kept):
     slab = n // RADIX
     return (
         n == RADIX * slab
-        and slab > 1
+        and slab == 4
         and chans == 8
         and chans % slab == 0
         and local % (BLOCKS * RADIX * 8) == 0
@@ -396,7 +513,8 @@
         and raw % LANES == 0
         and raw <= 8 * LANES
         and uniq % LANES == 0
-        and 2 * LANES <= uniq <= 4 * LANES
+        and uniq == 4 * LANES
+        and local == LANES
         and kept == 16
         and chans // slab == 2
     )
@@ -412,26 +530,22 @@
     steps = tiles * per_dev
     per = local // RADIX
     width = 2 * chans
-    tb = local // BLOCKS
     rank, enc, dec = stacked_tables(slab, local)
     total = 2 * rank
     vmem = pl.BlockSpec(memory_space=pltpu.VMEM)
     hbm = pl.BlockSpec(memory_space=pl.ANY)
     f32, bf16 = jnp.float32, jnp.bfloat16
     dma = pltpu.SemaphoreType.DMA
-    group = 16
-    mmodes, flat = pl.pallas_call(
+    stride = 2 * kept
+    mm, modes = pl.pallas_call(
         functools.partial(fused_kernel, n, local, chans, uniq, kept, rank),
         out_shape=(
-            jax.ShapeDtypeStruct((local * width, uniq), f32),
-            jax.ShapeDtypeStruct((local // group, 1, group * 2 * kept), f32),
+            pltpu.VMEM((tiles, local * width, LANES), f32),
+            pltpu.VMEM((2, kept, local), f32),
         ),
-        in_specs=[hbm] * 4 + [vmem],
-        out_specs=(hbm, vmem),
+        in_specs=[hbm] * 4 + [vmem] * 2,
+        out_specs=(pl.BlockSpec(memory_space=pltpu.VMEM), vmem),
         scratch_shapes=[
-            pltpu.VMEM((BLOCKS, RADIX, tb // RADIX, width, raw), f32),
-            pltpu.VMEM((uniq, raw), bf16),
-            pltpu.VMEM((tiles, tb * width, LANES), f32),
             pltpu.VMEM((steps, slab, RADIX, 2, per, LANES), f32),
             pltpu.VMEM((steps, slab, RADIX, 2, per, LANES), f32),
             pltpu.VMEM((RADIX, total, LANES), f32),
@@ -439,35 +553,42 @@
             pltpu.VMEM((steps, RADIX, total, LANES), f32),
             pltpu.VMEM((RADIX, dec.shape[2], LANES), f32),
             pltpu.VMEM((steps, slab, RADIX, 2, per, LANES), f32),
-            pltpu.VMEM((tiles, local * width, LANES), f32),
-            pltpu.VMEM((local, 2, kept, LANES), f32),
-            pltpu.VMEM((2, local, 2, kept, chans, LANES), bf16),
+            pltpu.VMEM((local * stride, LANES), f32),
+            pltpu.VMEM((2, kept * chans, LANES), f32),
             pltpu.VMEM(enc.shape, bf16),
             pltpu.VMEM(dec.shape, bf16),
-            dma((BLOCKS, RADIX)),
+            dma((BLOCKS,)),
             dma((2,)),
-            dma((BLOCKS, slab)),
-            dma((BLOCKS, slab)),
-            dma((steps, slab)),
-            dma((steps, slab)),
-            dma((steps, RADIX)),
-            dma((steps, RADIX)),
-            dma((steps, slab)),
-            dma((steps, slab)),
-            dma((2,)),
-            dma((tiles,)),
+            dma((steps,)),
+            dma((steps,)),
+            dma,
+            dma((steps,)),
+            dma,
+            dma((steps,)),
+            dma((SLOTS,)),
         ],
         compiler_params=pltpu.CompilerParams(
-            collective_id=0, has_side_effects=True, vmem_limit_bytes=67043328 - 2**17
+            collective_id=0, has_side_effects=True, vmem_limit_bytes=59 * 2**20
         ),
         name="fused",
     )(
         visibilities.reshape(local // RADIX, RADIX, width, raw),
-        filters, enc, dec, redundancy.reshape(1, raw),
-    )
-    coefs = flat.reshape(local, 2, kept)
-    kept_mask = lax.broadcasted_iota(jnp.int32, (local, kept), 1) < mode_counts[:, None]
-    return mmodes.reshape(local, 2, chans, uniq), jnp.where(kept_mask[:, None, :], coefs, 0.0)
+        filters, enc, dec, redundancy.reshape(1, raw), mode_counts.reshape(1, local),
+    )
+    chunks = 8
+    mmodes, modes = pl.pallas_call(
+        emit_kernel,
+        out_shape=(
+            jax.ShapeDtypeStruct((local * width, uniq), f32),
+            jax.ShapeDtypeStruct((2, kept, local), f32),
+        ),
+        in_specs=[vmem, vmem],
+        out_specs=(hbm, vmem),
+        scratch_shapes=[dma((tiles, chunks))],
+        compiler_params=pltpu.CompilerParams(vmem_limit_bytes=32 * 2**20),
+        name="emit",
+    )(mm, modes)
+    return mmodes.reshape(local, 2, chans, uniq), jnp.transpose(modes, (2, 0, 1))
 
 
 def phase_table(numer, period):

time: 152 us -> 132 us (0.87)
  Pallas kernels: 143 us -> 131 us
  local copies, waits for them, and re-layouts: 5.94 us -> 0 us
    pallas_call x1, Pallas kernels: 143 us -> 128 us  [fused_device(): pl.pallas_call(functools.partial(fused_kernel, n, local, chans, uniq, kep...]
    unnamed x4 -> x0, local copies, waits for them, and re-layouts: 5.73 us -> none
    pallas_call x0 -> x1, Pallas kernels: none -> 2.87 us  [fused_device(): pl.pallas_call(emit_kernel, out_shape=(jax.ShapeDtypeStruct((local * widt...]
where the time goes in v2:
time: 132 us; the launch traced here: 131 us
  Pallas kernels  131 us (99%)
    pallas_call x1, Pallas kernels, fused_device(): pl.pallas_call(functools.partial(fused_kernel, n, local, chans, uniq, kep...  128 us
    pallas_call x1, Pallas kernels, fused_device(): pl.pallas_call(emit_kernel, out_shape=(jax.ShapeDtypeStruct((local * widt...  2.87 us

profile of v2, /device:TPU:13, one launch (start us, length us, event | category | flops | bytes accessed | tf_op | source)
XLA Modules:
  0.0 131.3 jit_solution(7914264634201376691)
XLA Ops:
  0.6 127.8 %fused.1 = (f32[4,2048,128]{2,1,0:T(8,128)S(1)}, f32[2,16,128]{2,1,0:T(8,128)S(1)}) custom-call(f32[32,4,16,1024]{3,2,1,0:T(8,128)} %bitcast.5, bf16[128,2,16,8,512]{4,3,2,1,0:T(8,128)(2,1)} %filt_ref.1, bf16[4,608,256]{2,1,0:T(8,128)(2,1)} %constant.4.clone.enc_hbm, bf16[4,512,384]{2,1,0:T(8,128)(2,1)} %constant.5.clone.dec_hbm, s32[1,1024]{1,0:T(1,128)} %bitcast.6, ...), custom_call_target="tpu_custom_call" | custom-call | tf_op jit(solution)/shard_map/fused/pallas_call | solution.py:540
  128.5 2.9 %emit.1 = (f32[2048,512]{1,0:T(8,128)}, f32[2,16,128]{2,1,0:T(8,128)}) custom-call(f32[4,2048,128]{2,1,0:T(8,128)S(1)} %get-tuple-element.6.mm_ref, f32[2,16,128]{2,1,0:T(8,128)S(1)} %get-tuple-element.7.modes_ref), custom_call_target="tpu_custom_call" | custom-call | tf_op jit(solution)/shard_map/emit/pallas_call | solution.py:579

commit v3 on v2

--- a/solution.py
+++ b/solution.py
@@ -13,7 +13,7 @@
 BLOCKS = 4
 RADIX = 4
 AHEAD = 3
-SLOTS = 3
+GROUP = 16
 NT = (((1,), (1,)), ((), ()))
 
 
@@ -128,7 +128,7 @@
 def fused_kernel(
     n, local, chans, uniq, kept, rank,
     vis_ref, filt_ref, enc_hbm, dec_hbm, red_ref, counts_ref, mm_ref, modes_ref,
-    send, recv_a, mix, send_b, recv_b, back, recv_c, part, turned, enc, dec,
+    send, recv, mix, send_b, recv_b, back, part, turned, enc, dec,
     load_sem, tab_sem, as_, ar, bs, br, cs, cr, filt_sem,
 ):
     slab = n // RADIX
@@ -155,6 +155,12 @@
 
     barrier = pltpu.get_barrier_semaphore()
     peers = [in_slab(o) for o in range(1, slab)] + [across(o) for o in range(1, RADIX)]
+    odd = lax.rem(c, 2)
+    near, ahead, behind = 1 + 2 * odd, 2 - odd, 3 - odd
+
+    def slot(s):
+        return lax.rem(s + steps, steps + 2)
+
     def remote(src, dst, ssem, rsem, peer):
         return pltpu.make_async_remote_copy(
             src_ref=src, dst_ref=dst, send_sem=ssem, recv_sem=rsem,
@@ -165,13 +171,13 @@
         at = pl.ds(i * vb if isinstance(i, int) else pl.multiple_of(i * vb, vb), vb)
         dest = lax.rem(c + o, slab)
         return remote(
-            send.at[0, dest, :, :, at, :], recv_a.at[0, c, :, :, at, :],
+            send.at[0, dest, :, :, at, :], recv.at[0, c, :, :, at, :],
             as_.at[0], ar.at[0], in_slab(o),
         )
 
     def first(s, o):
         dest = lax.rem(c + o, slab)
-        return remote(send.at[s, dest], recv_a.at[s, c], as_.at[s], ar.at[s], in_slab(o))
+        return remote(send.at[s, dest], recv.at[s, c], as_.at[s], ar.at[s], in_slab(o))
 
     def second(s, o):
         dest = lax.rem(z + o, RADIX)
@@ -179,7 +185,7 @@
 
     def all_first(s):
         some = pl.ds(0, slab - 1)
-        return remote(send.at[s, some], recv_a.at[s, some], as_.at[s], ar.at[s], in_slab(1))
+        return remote(send.at[s, some], recv.at[s, some], as_.at[s], ar.at[s], in_slab(1))
 
     def all_second(s):
         some = pl.ds(0, RADIX - 1)
@@ -187,15 +193,20 @@
 
     def all_third(s):
         some = pl.ds(0, slab - 1)
-        return remote(send.at[s, some], recv_c.at[s, some], cs, cr.at[s], in_slab(1))
+        return remote(send.at[s, some], recv.at[slot(s), some], cs, cr.at[s], in_slab(1))
+
+    def last_third(blocks, late):
+        s, some = steps - 1, pl.ds(0, blocks)
+        return remote(send.at[s, some], recv.at[slot(s), some], cs, cr.at[s + late], in_slab(1))
 
     def third(s, o):
         dest = lax.rem(c + o, slab)
-        return remote(send.at[s, dest], recv_c.at[s, c], cs, cr.at[s], in_slab(o))
+        far = lax.div(s, steps - 1) * (o != near).astype(jnp.int32)
+        return remote(send.at[s, dest], recv.at[slot(s), c], cs, cr.at[s + far], in_slab(o))
 
     def encode(s):
         for r in range(RADIX):
-            x = recv_a[s, :, r].reshape(slab * 2 * per, LANES)
+            x = recv[s, :, r].reshape(slab * 2 * per, LANES)
             mix[r] = stacked_dot(enc[r], x)[:mix.shape[1]]
 
         def put(k, at, v):
@@ -205,9 +216,6 @@
         recv_b[s, z] = send_b[s, z]
         for o in range(1, RADIX):
             second(s, o).start()
-
-    odd = lax.rem(c, 2)
-    near, ahead, behind = 1 + 2 * odd, 2 - odd, 3 - odd
 
     def averages(vis_buf, wt, avg):
         def load(i, r):
@@ -266,13 +274,14 @@
         lax.fori_loop(0, BLOCKS, early, 0)
         for i in range(BLOCKS):
             first_part(i, behind).start()
-        recv_a[0, c] = send[0, c]
+        recv[0, c] = send[0, c]
         for copy in table_copies:
             copy.wait()
         all_first(0).wait_recv()
         for s in (1, 2):
             for o in range(1, slab):
                 first(s, o).start()
+
         encode(0)
 
         def more(i, carry):
@@ -291,17 +300,17 @@
     pl.run_scoped(
         functools.partial(
             transform_kernel, n, local, chans, uniq, kept, rank, filt_ref, counts_ref, mm_ref, modes_ref,
-            send, recv_a, mix, send_b, recv_b, back, recv_c, part, turned, enc, dec,
-            first, second, third, all_first, all_second, all_third, encode, filt_sem,
+            send, recv, mix, send_b, recv_b, back, part, turned, enc, dec,
+            first, second, third, all_first, all_second, all_third, last_third, encode, slot, filt_sem,
         ),
-        pltpu.VMEM((SLOTS, local, 2, kept, chans, LANES), jnp.bfloat16),
+        pltpu.VMEM((tiles, local, 2, kept, chans, LANES), jnp.bfloat16),
     )
 
 
 def transform_kernel(
     n, local, chans, uniq, kept, rank, filt_ref, counts_ref, mm_ref, modes_ref,
-    send, recv_a, mix, send_b, recv_b, back, recv_c, part, turned, enc, dec,
-    first, second, third, all_first, all_second, all_third, encode, filt_sem, filt,
+    send, recv, mix, send_b, recv_b, back, part, turned, enc, dec,
+    first, second, third, all_first, all_second, all_third, last_third, encode, slot, filt_sem, filt,
 ):
     slab = n // RADIX
     me = lax.axis_index("tm")
@@ -316,16 +325,15 @@
 
     def fetch(j):
         at = pl.multiple_of(j * LANES, LANES)
-        slot = lax.rem(j, SLOTS)
         return pltpu.make_async_copy(
-            filt_ref.at[:, :, :, :, pl.ds(at, LANES)], filt.at[slot], filt_sem.at[slot]
+            filt_ref.at[:, :, :, :, pl.ds(at, LANES)], filt.at[j], filt_sem.at[j]
         )
 
-    for j in range(SLOTS):
+    for j in range(tiles):
         fetch(j).start()
 
     def keep(s, carry):
-        recv_a[s, c] = send[s, c]
+        recv[s, c] = send[s, c]
         return carry
 
     lax.fori_loop(1, steps, keep, 0)
@@ -341,62 +349,62 @@
             y = stacked_dot(dec[r], back[r]).reshape(slab, 2, per, LANES)
             for d in range(slab):
                 send[s, d, r] = y[d]
-        recv_c[s, c] = send[s, c]
+        recv[slot(s), c] = send[s, c]
         for o in range(1, slab):
             third(s, o).start()
 
     def place(s, j, f2):
         all_third(s).wait_recv()
-
+        spread(s, j, f2, 0, slab)
+
+    def spread(s, j, f2, low, high):
         def one(d, carry):
             for r in range(RADIX):
                 for p in range(2):
                     start = (r * 2 + p) * chans + f2 + d * per_dev
-                    mm_ref[j, pl.ds(start, per, stride=RADIX * width), :] = recv_c[s, d, r, p]
+                    mm_ref[j, pl.ds(start, per, stride=RADIX * width), :] = recv[slot(s), d, r, p]
             return carry
 
-        lax.fori_loop(0, slab, one, 0)
+        lax.fori_loop(low, high, one, 0)
 
     def turn(j):
-        slot = lax.rem(j, SLOTS)
         fetch(j).wait()
 
         def one(m, carry):
             for p in range(2):
-                turned[p] = filt[slot, m, p].astype(jnp.float32).reshape(kept * chans, LANES)
+                turned[p] = filt[j, m, p].astype(jnp.float32).reshape(kept * chans, LANES)
             for p in range(2):
                 for f in range(chans):
                     for g in range(kept // 8):
                         rows = turned[p, pl.ds(g * 8 * chans + f, 8, stride=chans), :]
-                        filt[slot, m, p, f * (kept // 8) + g] = rows.astype(jnp.bfloat16)
+                        filt[j, m, p, f * (kept // 8) + g] = rows.astype(jnp.bfloat16)
             return carry
 
         lax.fori_loop(0, local, one, 0)
 
-    def project(j, f2, m):
-        slot = lax.rem(j, SLOTS)
+    def project(j, f2, m, sources):
         per_chan = kept // 8
         re = pl.ds(pl.multiple_of(m * stride, 8), kept)
         im = pl.ds(pl.multiple_of(m * stride + kept, 8), kept)
         real, imag = part[re, :], part[im, :]
-        for d in range(slab):
+        for d in sources:
             f = d * per_dev + f2
             at = f * per_chan
             x0 = mm_ref[j, pl.ds(m * width + f, 1), :].astype(jnp.bfloat16).astype(jnp.float32)
             x1 = mm_ref[j, pl.ds(m * width + chans + f, 1), :].astype(jnp.bfloat16).astype(jnp.float32)
-            f0 = filt[slot, m, 0, pl.ds(at, per_chan)].astype(jnp.float32).reshape(kept, LANES)
-            f1 = filt[slot, m, 1, pl.ds(at, per_chan)].astype(jnp.float32).reshape(kept, LANES)
+            f0 = filt[j, m, 0, pl.ds(at, per_chan)].astype(jnp.float32).reshape(kept, LANES)
+            f1 = filt[j, m, 1, pl.ds(at, per_chan)].astype(jnp.float32).reshape(kept, LANES)
             real += f0 * x0 - f1 * x1
             imag += f0 * x1 + f1 * x0
         part[re, :] = real
         part[im, :] = imag
 
-    def projects(j, f2, low, high):
+    def projects(j, f2, sources):
         def one(m, carry):
-            project(j, f2, m)
+            project(j, f2, m, sources)
             return carry
 
-        lax.fori_loop(low, high, one, 0, unroll=2)
+        lax.fori_loop(0, local, one, 0, unroll=2)
 
     back[:, total:, :] = jnp.zeros((RADIX, back.shape[1] - total, LANES), jnp.float32)
 
@@ -413,25 +421,23 @@
     for e in range(1, AHEAD):
         later(e)
 
+    turn(0)
+
     def step(d, carry):
-        @pl.when(d < SLOTS)
+        @pl.when((d == 1) | (d == 2))
         def _():
             turn(d)
+
+        @pl.when(d == 1)
+        def _():
+            turn(tiles - 1)
 
         @pl.when(d >= 2)
         def _():
             j, f2 = lax.div(d - 2, per_dev), lax.rem(d - 2, per_dev)
             place(d - 2, j, f2)
 
-            projects(j, f2, 0, local)
-
-            @pl.when((f2 == per_dev - 1) & (j + SLOTS < tiles))
-            def _():
-                fetch(j + SLOTS).start()
-
-        @pl.when((d >= steps - 2) & (d - (steps - 2) + SLOTS < tiles))
-        def _():
-            turn(d - (steps - 2) + SLOTS)
+            projects(j, f2, range(slab))
 
         all_first(d).wait_send()
         decode(d)
@@ -449,30 +455,47 @@
 
     def gather(q, outs):
         outs = list(outs)
-        for i in range(8):
-            m = q * 8 + i
+        for i in range(GROUP):
+            m = q * GROUP + i
             for p in range(2):
                 at = pl.ds(pl.multiple_of(m * stride + p * kept, 8), kept)
                 row = jnp.sum(part[at, :], axis=1, keepdims=True)
                 outs[p] = jnp.where(lane == m, row, outs[p])
         return tuple(outs)
 
-    def last(q, outs):
-        outs = gather(jnp.maximum(q - 1, 0), outs)
-        for i in range(8):
-            project(j, per_dev - 1, q * 8 + i)
-        return outs
-
-    for f2 in range(per_dev):
+    for f2 in range(per_dev - 1):
         place(j * per_dev + f2, j, f2)
-        if f2 < per_dev - 1:
-            projects(j, f2, 0, local)
+        projects(j, f2, range(slab))
+    f2 = per_dev - 1
+    half = slab // 2
+    order = lax.broadcasted_iota(jnp.int32, (kept, LANES), 0)
     zero = jnp.zeros((kept, LANES), jnp.float32)
-    outs = lax.fori_loop(0, local // 8, last, (zero, zero))
-    outs = gather(local // 8 - 1, outs)
-    order = lax.broadcasted_iota(jnp.int32, (kept, LANES), 0)
-    for p in range(2):
-        modes_ref[p] = jnp.where(order < counts_ref[...], outs[p], 0.0)
+
+    def finish(early, late):
+        last_third(1, 0).wait_recv()
+        spread(steps - 1, j, f2, early[0], early[0] + half)
+        projects(j, f2, early)
+        last_third(2, 1).wait_recv()
+        spread(steps - 1, j, f2, late[0], late[0] + half)
+
+        def last(q, outs):
+            outs = gather(jnp.maximum(q - 1, 0), outs)
+            for i in range(GROUP):
+                project(j, f2, q * GROUP + i, late)
+            return outs
+
+        outs = lax.fori_loop(0, local // GROUP, last, (zero, zero))
+        outs = gather(local // GROUP - 1, outs)
+        for p in range(2):
+            modes_ref[p] = jnp.where(order < counts_ref[...], outs[p], 0.0)
+
+    @pl.when(lax.div(c, half) == 0)
+    def _():
+        finish(range(half), range(half, slab))
+
+    @pl.when(lax.div(c, half) == 1)
+    def _():
+        finish(range(half, slab), range(half))
 
     def drain(s, carry):
         all_second(s).wait_send()
@@ -547,12 +570,11 @@
         out_specs=(pl.BlockSpec(memory_space=pltpu.VMEM), vmem),
         scratch_shapes=[
             pltpu.VMEM((steps, slab, RADIX, 2, per, LANES), f32),
-            pltpu.VMEM((steps, slab, RADIX, 2, per, LANES), f32),
+            pltpu.VMEM((steps + 2, slab, RADIX, 2, per, LANES), f32),
             pltpu.VMEM((RADIX, total, LANES), f32),
             pltpu.VMEM((steps, RADIX, total, LANES), f32),
             pltpu.VMEM((steps, RADIX, total, LANES), f32),
             pltpu.VMEM((RADIX, dec.shape[2], LANES), f32),
-            pltpu.VMEM((steps, slab, RADIX, 2, per, LANES), f32),
             pltpu.VMEM((local * stride, LANES), f32),
             pltpu.VMEM((2, kept * chans, LANES), f32),
             pltpu.VMEM(enc.shape, bf16),
@@ -564,11 +586,11 @@
             dma,
             dma((steps,)),
             dma,
-            dma((steps,)),
-            dma((SLOTS,)),
+            dma((steps + 1,)),
+            dma((tiles,)),
         ],
         compiler_params=pltpu.CompilerParams(
-            collective_id=0, has_side_effects=True, vmem_limit_bytes=59 * 2**20
+            collective_id=0, has_side_effects=True, vmem_limit_bytes=62_700_000
         ),
         name="fused",
     )(

time: 132 us -> 131 us (level)
  no operation moved by 1% of the time
where the time goes in v3:
time: 131 us
  Pallas kernels  130 us (99%)
    pallas_call x1, Pallas kernels, fused_device(): pl.pallas_call(functools.partial(fused_kernel, n, local, chans, uniq, kep...  127 us
    pallas_call x1, Pallas kernels, fused_device(): pl.pallas_call(emit_kernel, out_shape=(jax.ShapeDtypeStruct((local * widt...  2.87 us

profile of v3, /device:TPU:13, one launch (start us, length us, event | category | flops | bytes accessed | tf_op | source)
XLA Modules:
  0.0 130.5 jit_solution(12611153606242593556)
XLA Ops:
  0.6 127.0 %fused.1 = (f32[4,2048,128]{2,1,0:T(8,128)S(1)}, f32[2,16,128]{2,1,0:T(8,128)S(1)}) custom-call(f32[32,4,16,1024]{3,2,1,0:T(8,128)} %bitcast.5, bf16[128,2,16,8,512]{4,3,2,1,0:T(8,128)(2,1)} %filt_ref.1, bf16[4,608,256]{2,1,0:T(8,128)(2,1)} %constant.4.clone.enc_hbm, bf16[4,512,384]{2,1,0:T(8,128)(2,1)} %constant.5.clone.dec_hbm, s32[1,1024]{1,0:T(1,128)} %bitcast.6, ...), custom_call_target="tpu_custom_call" | custom-call | tf_op jit(solution)/shard_map/fused/pallas_call | solution.py:563
  127.6 2.9 %emit.1 = (f32[2048,512]{1,0:T(8,128)}, f32[2,16,128]{2,1,0:T(8,128)}) custom-call(f32[4,2048,128]{2,1,0:T(8,128)S(1)} %get-tuple-element.6.mm_ref, f32[2,16,128]{2,1,0:T(8,128)S(1)} %get-tuple-element.7.modes_ref), custom_call_target="tpu_custom_call" | custom-call | tf_op jit(solution)/shard_map/emit/pallas_call | solution.py:601

commit v4 on v3

--- a/solution.py
+++ b/solution.py
@@ -223,31 +223,36 @@
                 vis_ref.at[pl.ds(i * vb, vb), r], vis_buf.at[i, r], load_sem.at[i]
             )
 
-        for i in range(2):
-            for r in range(RADIX):
-                load(i, r).start()
+        for r in range(RADIX):
+            load(0, r).start()
         for peer in peers:
             pl.semaphore_signal(barrier, inc=1, device_id={"tm": peer}, device_id_type=MESH)
-        wt[...] = (
-            lax.broadcasted_iota(jnp.int32, wt.shape, 0) == red_ref[...]
-        ).astype(jnp.float32).astype(jnp.bfloat16)
-        ones = jnp.ones((8, wt.shape[1]), jnp.bfloat16)
-        for i in range(2, BLOCKS):
-            for r in range(RADIX):
-                load(i, r).start()
-        for copy in table_copies:
-            copy.start()
-        counts = lax.dot_general(ones, wt[...], NT, preferred_element_type=jnp.float32)
-        inverse = 1.0 / counts[0:1]
-
-        def average(i, h):
+        def members_of(h):
+            rows = slice(h * 2 * LANES, (h + 1) * 2 * LANES)
+            shape = (2 * LANES, wt.shape[1])
+            wt[rows, :] = (
+                lax.broadcasted_iota(jnp.int32, shape, 0) + h * 2 * LANES == red_ref[...]
+            ).astype(jnp.float32).astype(jnp.bfloat16)
+
+        def inverse_of(h):
+            rows = slice(h * 2 * LANES, (h + 1) * 2 * LANES)
+            ones = jnp.ones((8, wt.shape[1]), jnp.bfloat16)
+            counts = lax.dot_general(ones, wt[rows, :], NT, preferred_element_type=jnp.float32)
+            return 1.0 / counts[0:1]
+
+        members_of(0)
+        for r in range(RADIX):
+            load(1, r).start()
+        inverse = inverse_of(0)
+
+        def average(i, h, inverse):
             at = pl.ds(i * vb if isinstance(i, int) else pl.multiple_of(i * vb, vb), vb)
             high, low = split_bf16(vis_buf[i].reshape(tb * width, vis_buf.shape[-1]))
             lanes = slice(h * 2 * LANES, (h + 1) * 2 * LANES)
             members = wt[lanes, :]
             summed = lax.dot_general(high, members, NT, preferred_element_type=jnp.float32)
             summed += lax.dot_general(low, members, NT, preferred_element_type=jnp.float32)
-            mean = summed * inverse[:, lanes]
+            mean = summed * inverse
             for q in range(2):
                 avg[q] = mean[:, q * LANES:(q + 1) * LANES]
             for q in range(2):
@@ -261,7 +266,12 @@
 
         def early(i, carry):
             pltpu.make_async_copy(vis_buf.at[i], vis_buf.at[i], load_sem.at[i]).wait()
-            average(i, 0)
+            @pl.when(i + 2 < BLOCKS)
+            def _():
+                for r in range(RADIX):
+                    load(i + 2, r).start()
+
+            average(i, 0, inverse)
 
             @pl.when(i == 0)
             def _():
@@ -272,6 +282,8 @@
             return carry
 
         lax.fori_loop(0, BLOCKS, early, 0)
+        for copy in table_copies:
+            copy.start()
         for i in range(BLOCKS):
             first_part(i, behind).start()
         recv[0, c] = send[0, c]
@@ -284,8 +296,11 @@
 
         encode(0)
 
+        members_of(1)
+        inverse_rest = inverse_of(1)
+
         def more(i, carry):
-            average(i, 1)
+            average(i, 1, inverse_rest)
             return carry
 
         lax.fori_loop(0, BLOCKS, more, 0)

time: 131 us -> 131 us (level)
  no operation moved by 1% of the time
where the time goes in v4:
time: 131 us
  Pallas kernels  130 us (99%)
    pallas_call x1, Pallas kernels, fused_device(): pl.pallas_call(functools.partial(fused_kernel, n, local, chans, uniq, kep...  127 us
    pallas_call x1, Pallas kernels, fused_device(): pl.pallas_call(emit_kernel, out_shape=(jax.ShapeDtypeStruct((local * widt...  2.87 us

profile of v4, /device:TPU:13, one launch (start us, length us, event | category | flops | bytes accessed | tf_op | source)
XLA Modules:
  0.0 130.6 jit_solution(646834424745458291)
XLA Ops:
  0.6 127.1 %fused.1 = (f32[4,2048,128]{2,1,0:T(8,128)S(1)}, f32[2,16,128]{2,1,0:T(8,128)S(1)}) custom-call(f32[32,4,16,1024]{3,2,1,0:T(8,128)} %bitcast.5, bf16[128,2,16,8,512]{4,3,2,1,0:T(8,128)(2,1)} %filt_ref.1, bf16[4,608,256]{2,1,0:T(8,128)(2,1)} %constant.4.clone.enc_hbm, bf16[4,512,384]{2,1,0:T(8,128)(2,1)} %constant.5.clone.dec_hbm, s32[1,1024]{1,0:T(1,128)} %bitcast.6, ...), custom_call_target="tpu_custom_call" | custom-call | tf_op jit(solution)/shard_map/fused/pallas_call | solution.py:578
  127.7 2.9 %emit.1 = (f32[2048,512]{1,0:T(8,128)}, f32[2,16,128]{2,1,0:T(8,128)}) custom-call(f32[4,2048,128]{2,1,0:T(8,128)S(1)} %get-tuple-element.6.mm_ref, f32[2,16,128]{2,1,0:T(8,128)S(1)} %get-tuple-element.7.modes_ref), custom_call_target="tpu_custom_call" | custom-call | tf_op jit(solution)/shard_map/emit/pallas_call | solution.py:616
